TPU v7x, 32 devices: a whole 2x2x4 slice. The times are simulated.
32 devices in a mesh: row: 8 (over z, core), col: 4 (over y, x).
Axes of the slice: x: 2, y: 2, z: 4, core: 2. Of those that a mesh axis runs over, the one named last changes fastest.
Arguments:
- pair_exchange: bfloat16 [64, 16, 1024], P(('row', 'col')), may hold values from -6 to 6
- conduction: bfloat16 [64, 4, 1024], P(('row', 'col')), may hold values from -6 to 6
- valence: bfloat16 [64, 4, 1024], P(('row', 'col')), may hold values from -6 to 6
- coulomb: float32 [1024], replicated, may hold values from 0.5 to 5
- screening: float32 [34, 1024], replicated, may hold values from 0.1 to 1
- energies: float32 [64, 16], P(('row', 'col')), may hold values from 1 to 9
- vectors: bfloat16 [64, 512], P(('row', 'col')), may hold values from -6 to 6
- k_coords: int32 [64, 2], P(('row', 'col')), may hold values from 0 to 31, as said below
Outputs:
- residual_block: float32 [64, 512], P(('row', 'col'))
- alpha: float32 [32, 32], replicated
Inputs may be any that keep to these rules, and one draw needn't show every extreme that they name: `k_coords`: each row holds a k-point's coordinates on the periodic 32 x 2 mesh, first then second; every mesh point occurs exactly once.
All inputs are finite; a program needn't handle non-finite values.
Results may differ from a plain program's by a relative error of at most 0.0028.
Values may be sent and summed in bfloat16 or wider, within the bound.
A program may use at most 64 MiB of HBM per device.

v0:
```python
import functools

import jax
import jax.numpy as jnp
from jax import lax
from jax.experimental import pallas as pl
from jax.experimental.pallas import tpu as pltpu
from jax.sharding import PartitionSpec as P

MX = 32
LANES = 128
MESH = pl.DeviceIdType.MESH
F32 = jnp.float32
BF16 = jnp.bfloat16


def split_pair(value):
    high = value.astype(BF16)
    return high, (value - high.astype(F32)).astype(BF16)


def dot(a, b, contract):
    return lax.dot_general(a, b, ((contract[0:1], contract[1:2]), ((), ())), preferred_element_type=F32)


def iota(shape, axis):
    return lax.broadcasted_iota(jnp.int32, shape, axis)


def one_hot(condition):
    return jnp.where(condition, 1.0, 0.0).astype(BF16)


def kernel(
    dims, px_hbm, cond_hbm, val_hbm, coulomb_hbm, screening_hbm, vec_hbm, energy_hbm, place_hbm,
    out_ref, alpha_ref,
    px_ref, cond_ref, val_ref, coulomb_ref, screening_ref, vec_ref, energy_ref, place_ref, msg_ref, wide_ref, load_sem,
    slots, px_slots, sel_v, sel_c, tile_m, block_m, perm, sel_k, screen, tiled, pairs, proj, coords, coupling,
    dens_slots, partial, out_send, out_slots, gram_slots,
    in_send, in_recv, px_send, px_recv, dens_send, dens_recv, gram_send, gram_recv, o_send, o_recv,
):
    rows, cols, nk, nv, nc, nvec, total, mesh_cols = dims
    row, col = lax.axis_index("row"), lax.axis_index("col")
    me = row * cols + col
    count = rows * cols
    kb = rows * nk
    nb = nv * nc
    unit = nk * nv
    per = kb * nv
    batch = per * nc

    def other(step):
        peer = lax.rem(me + step, count)
        return peer // cols, lax.rem(peer, cols)

    barrier = pltpu.get_barrier_semaphore()

    for step in range(1, rows):
        pl.semaphore_signal(barrier, inc=1, device_id=(lax.rem(row + step, rows), col), device_id_type=MESH)
    for step in range(1, cols):
        pl.semaphore_signal(barrier, inc=1, device_id=(row, lax.rem(col + step, cols)), device_id_type=MESH)

    mine = pl.ds(pl.multiple_of(row * LANES, LANES), LANES)
    loads = [
        pltpu.make_async_copy(src, dst, load_sem.at[at])
        for at, (src, dst) in enumerate((
            (val_hbm, val_ref), (cond_hbm, cond_ref), (vec_hbm, vec_ref), (place_hbm, place_ref), (energy_hbm, energy_ref), (px_hbm, px_ref),
            (screening_hbm.at[:, mine], screening_ref), (coulomb_hbm.at[:, mine], coulomb_ref)))
    ]
    for load in loads:
        load.start()
    for load in loads[:5]:
        load.wait()
    row8 = iota((8, LANES), 0)
    lane8 = iota((8, LANES), 1)
    spots = jnp.zeros((8, LANES), F32)
    for axis in range(2):
        for k in range(nk):
            spots = jnp.where(row8 == axis * nk + k, place_ref[k, axis].astype(F32), spots)
    energy = jnp.zeros((8, LANES), F32)
    for k in range(nk):
        for t in range(nb):
            energy = jnp.where((row8 == k * nv + t // nc) & (lane8 // nvec == t % nc), energy_ref[k, t], energy)
    vec = vec_ref[...].astype(F32)
    packed_own = jnp.concatenate(
        [vec[k:k + 1, j * LANES:(j + 1) * LANES] for k in range(nk) for j in range(nv)], axis=0)
    wide_ref[0] = packed_own
    wide_ref[1] = energy * packed_own
    message = jnp.concatenate(
        [ref[k].astype(F32) for k in range(nk) for ref in (val_ref, cond_ref)], axis=0).astype(BF16)
    extra = jnp.concatenate([packed_own, spots], axis=0).astype(BF16)
    for r in range(rows):
        msg_ref[r, 0:16] = message[:, r * LANES:(r + 1) * LANES]
        msg_ref[r, 16:32] = extra

    at = iota((batch, rows * 16), 0)
    to = iota((batch, rows * 16), 1)
    base = (at // unit) % rows * 16 + (at // nv) % nk * 8
    sel_v[...] = one_hot(to == base + at % nv)
    sel_c[...] = one_hot(to == base + nv + at // per)
    at = iota((LANES, nc * LANES), 0)
    to = iota((LANES, nc * LANES), 1)
    tile_m[...] = one_hot((at // nvec == to // LANES) & (at % nvec == to % nvec))
    at = iota((batch, kb * nvec), 0)
    to = iota((batch, kb * nvec), 1)
    block_m[...] = one_hot((at // nv) % kb == to // nvec)
    at = iota((batch, rows * nk * nb), 0)
    to = iota((batch, rows * nk * nb), 1)
    perm[...] = one_hot(to == (at // nv) % kb * nb + at % nv * nc + at // per)
    at = iota((2 * cols * kb, count * 8), 0)
    to = iota((2 * cols * kb, count * 8), 1)
    point = at % (cols * kb)
    sel_k[...] = one_hot(to == point // nk * 8 + at // (cols * kb) * nk + point % nk)
    for load in loads[5:]:
        load.wait()
    slots[col, row] = msg_ref[row]
    high, low = split_pair(jnp.concatenate(
        [screening_ref[...], jnp.zeros((LANES - screening_ref.shape[0], LANES), F32)], axis=0))
    screen[0:LANES] = high
    screen[LANES:2 * LANES] = low

    pl.semaphore_wait(barrier, rows + cols - 2)

    def in_copy(step):
        pr = lax.rem(row + step, rows)
        return pltpu.make_async_remote_copy(
            src_ref=msg_ref.at[pr, 0:28], dst_ref=slots.at[col, row, 0:28],
            send_sem=in_send.at[col, pr], recv_sem=in_recv.at[col, row],
            device_id=(pr, col), device_id_type=MESH)

    def across(step):
        far = lax.rem(col // 2 + step // 2, cols // 2)
        return far * 2 + lax.rem(lax.rem(col, 2) + lax.rem(step, 2), 2)

    def relay_copy(r, step):
        pc = across(step)
        return pltpu.make_async_remote_copy(
            src_ref=slots.at[col, r, 0:28], dst_ref=slots.at[col, r, 0:28],
            send_sem=in_send.at[pc, r], recv_sem=in_recv.at[col, r],
            device_id=(row, pc), device_id_type=MESH)

    def px_copy(step):
        pr = lax.rem(row + step, rows)
        return pltpu.make_async_remote_copy(
            src_ref=px_ref.at[:, :, pl.ds(pl.multiple_of(pr * LANES, LANES), LANES)], dst_ref=px_slots.at[row],
            send_sem=px_send.at[pr], recv_sem=px_recv.at[row],
            device_id=(pr, col), device_id_type=MESH)

    def dens_copy(step):
        pc = lax.rem(col + step, cols)
        return pltpu.make_async_remote_copy(
            src_ref=dens_slots.at[col], dst_ref=dens_slots.at[col],
            send_sem=dens_send.at[pc], recv_sem=dens_recv.at[col],
            device_id=(row, pc), device_id_type=MESH)

    def gram_copy(step):
        pr, pc = other(step)
        return pltpu.make_async_remote_copy(
            src_ref=gram_slots.at[me], dst_ref=gram_slots.at[me],
            send_sem=gram_send.at[pr * cols + pc], recv_sem=gram_recv.at[me],
            device_id=(pr, pc), device_id_type=MESH)

    def o_copy(step):
        pr = lax.rem(row + step, rows)
        return pltpu.make_async_remote_copy(
            src_ref=out_send.at[pr], dst_ref=out_slots.at[row],
            send_sem=o_send.at[pr], recv_sem=o_recv.at[row],
            device_id=(pr, col), device_id_type=MESH)

    def start_all(copy, end):
        def body(step, carry):
            copy(step).start()
            return carry
        lax.fori_loop(1, end, body, 0)

    def landed(ref, sem):
        pltpu.make_async_copy(ref, ref, sem).wait()

    start_all(in_copy, rows)
    start_all(px_copy, rows)
    px_slots[row] = px_ref[:, :, mine]

    def relay(d, carry):
        r = lax.rem(row + d, rows)
        landed(slots.at[col, r, 0:28], in_recv.at[col, r])
        for step in range(1, cols):
            relay_copy(r, step).start()
        return carry

    for step in range(1, cols):
        relay_copy(row, step).start()
    lax.fori_loop(1, rows, relay, 0)

    def take_batch(which):
        got = slots[which]
        factors = got[:, 0:16, :].reshape(rows * 16, LANES)
        rest = got[:, 16:32, :].astype(F32)
        packed = rest[:, 0:8, :].reshape(per, LANES).astype(BF16)
        spots_in = rest[:, 8:16, :].reshape(rows * 8, LANES)
        coords[which] = jnp.where(iota(spots_in.shape, 0) % 8 < 4, spots_in, 0.0).astype(BF16)
        wide = dot(packed, tile_m[...], (1, 0)).astype(BF16)
        stacked = jnp.concatenate([wide[:, s * LANES:(s + 1) * LANES] for s in range(nc)], axis=0)
        tiled[which] = stacked
        joined = (dot(sel_v[...], factors, (1, 0)) * dot(sel_c[...], factors, (1, 0))).astype(BF16)
        pairs[which] = joined.astype(F32)
        spread = jnp.concatenate([stacked] * (kb * nvec // LANES), axis=1) * block_m[...]
        projected = dot(spread, joined, (0, 0))
        proj[pl.ds(which * kb, kb)] = projected.reshape(kb, nvec, LANES)

    take_batch(col)

    def px_wait(step, carry):
        r = lax.rem(row + step, rows)
        landed(px_slots.at[r], px_recv.at[r])
        return carry

    lax.fori_loop(1, rows, px_wait, 0)
    px = dot(perm[...], px_slots[...].reshape(rows * nk * nb, LANES), (1, 0)).astype(BF16)
    own_x = tiled[col][:, 0:nvec]
    dens_slots[col] = dot(own_x, px, (0, 0))
    start_all(dens_copy, cols)

    def rest_batches(step, carry):
        c = across(step)

        def wait_one(r, inner):
            landed(slots.at[c, r, 0:28], in_recv.at[c, r])
            return inner

        lax.fori_loop(0, rows, wait_one, 0)
        take_batch(c)
        return carry

    lax.fori_loop(1, cols, rest_batches, 0)

    place = dot(sel_k[...], coords[...].reshape(count * 8, LANES), (1, 0))
    points = cols * kb
    first, second = place[0:points], place[points:2 * points]
    lane = iota((points, LANES), 1).astype(F32)
    coupling[0, 0:points] = first
    coupling[1, 0:points] = second
    start = pl.multiple_of(col * kb, kb)
    own_first = coupling[0, pl.ds(start, kb), :]
    own_second = coupling[1, pl.ds(start, kb), :]
    hots = []
    for i in range(kb):
        da = jnp.abs(own_first[i:i + 1] - first)
        db = jnp.abs(own_second[i:i + 1] - second)
        q = jnp.minimum(da, MX - da) * (mesh_cols // 2 + 1) + jnp.minimum(db, mesh_cols - db)
        hots.append(one_hot(q == lane))
    for i in range(kb):
        coupling[i] = dot(jnp.concatenate([hots[i], hots[i]], axis=1), screen[...], (1, 0))

    def dens_wait(step, carry):
        c = lax.rem(col + step, cols)
        landed(dens_slots.at[c], dens_recv.at[c])
        return carry

    lax.fori_loop(1, cols, dens_wait, 0)
    density = dens_slots[0]
    for c in range(1, cols):
        density = density + dens_slots[c]
    high, low = split_pair(density * coulomb_ref[...] * (2.0 / (total * nb)))
    partial[...] = (dot(px, high, (1, 1)) + dot(px, low, (1, 1))).reshape(nc, rows, unit, nvec)

    wide_own = wide_ref[1]
    for s in range(nc):
        partial[s, row] = partial[s, row] + wide_own[:, s * nvec:(s + 1) * nvec]

    group = 4
    row_k = (iota((nc * unit, LANES), 0) // nv) % nk
    potentials = []
    for block in range(kb // group):
        def gather(j, sums):
            term = proj[j]
            return tuple(
                sums[u] + coupling[block * group + u, pl.ds(j, 1), :] * term for u in range(group))
        potentials += list(lax.fori_loop(
            0, points, gather, tuple(jnp.zeros((nvec, LANES), F32) for _ in range(group)), unroll=8))
    for r in range(rows):
        mine_pairs = pairs[col].reshape(nc, rows, unit, LANES)[:, r].reshape(nc * unit, LANES)
        left = jnp.concatenate(
            [jnp.where(row_k == k, mine_pairs, 0.0) for k in range(nk)], axis=1).astype(BF16)
        high, low = split_pair(jnp.concatenate([potentials[r * nk + k] for k in range(nk)], axis=1))
        direct = dot(left, high, (1, 1)) + dot(left, low, (1, 1))
        for s in range(nc):
            partial[s, r] = partial[s, r] - direct[s * unit:(s + 1) * unit] * (1.0 / total)

    whole = partial[...]
    packed = jnp.concatenate([whole[s].reshape(per, nvec) for s in range(nc)], axis=1)
    out_send[...] = packed.reshape(rows, unit, LANES)
    start_all(o_copy, rows)
    high, low = split_pair(whole.reshape(batch, nvec))
    gram = dot(own_x, high, (0, 0)) + dot(own_x, low, (0, 0))
    step = nvec // nc
    gram_slots[me] = jnp.concatenate([gram[s * step:(s + 1) * step] for s in range(nc)], axis=1)
    start_all(gram_copy, count)

    def o_wait(d, acc):
        r = lax.rem(row + d, rows)
        landed(out_slots.at[r], o_recv.at[r])
        return acc + out_slots[r]

    applied = lax.fori_loop(1, rows, o_wait, out_send[row])

    def gram_wait(d, carry):
        p = lax.rem(me + d, count)
        landed(gram_slots.at[p], gram_recv.at[p])
        return carry

    lax.fori_loop(1, count, gram_wait, 0)
    sums = jnp.sum(gram_slots[...], axis=0) * (1.0 / (total * nb))
    alpha = jnp.concatenate([sums[:, s * nvec:(s + 1) * nvec] for s in range(nc)], axis=0)
    alpha_ref[...] = alpha
    own = wide_ref[0]
    own_rows = jnp.concatenate([own[:, s * nvec:(s + 1) * nvec] for s in range(nc)], axis=0).astype(BF16)
    high, low = split_pair(alpha)
    taken = dot(own_rows, high, (1, 0)) + dot(own_rows, low, (1, 0))
    residual = applied - jnp.concatenate([taken[s * unit:(s + 1) * unit] for s in range(nc)], axis=1)
    for j in range(nv):
        out_ref[:, j * LANES:(j + 1) * LANES] = jnp.concatenate(
            [residual[k * nv + j:k * nv + j + 1] for k in range(nk)], axis=0)

    def drain(copy, end):
        def body(d, carry):
            copy(d).wait_send()
            return carry
        lax.fori_loop(1, end, body, 0)

    drain(in_copy, rows)

    def drain_relay(r, carry):
        for step in range(1, cols):
            relay_copy(r, step).wait_send()
        return carry

    lax.fori_loop(0, rows, drain_relay, 0)
    drain(px_copy, rows)
    drain(dens_copy, cols)
    drain(o_copy, rows)
    drain(gram_copy, count)


def fast_on_device(pair_exchange, conduction, valence, coulomb, screening, energies, vectors, k_coords):
    nk, nb, planes = pair_exchange.shape
    nv, nc = valence.shape[1], conduction.shape[1]
    nvec = vectors.shape[1] // nb
    rows, cols = lax.axis_size("row"), lax.axis_size("col")
    count = rows * cols
    total = nk * count
    unit = nk * nv
    kb = rows * nk
    batch = kb * nb
    vmem = pl.BlockSpec(memory_space=pltpu.VMEM)
    dma = pltpu.SemaphoreType.DMA
    points = cols * kb
    return pl.pallas_call(
        functools.partial(kernel, (rows, cols, nk, nv, nc, nvec, total, total // MX)),
        out_shape=(
            pltpu.VMEM((nk, nb * nvec), F32),
            pltpu.VMEM((nvec, nvec), F32),
        ),
        in_specs=[pl.BlockSpec(memory_space=pl.ANY)] * 8,
        out_specs=(vmem, vmem),
        scratch_shapes=[
            pltpu.VMEM(pair_exchange.shape, BF16),
            pltpu.VMEM(conduction.shape, BF16),
            pltpu.VMEM(valence.shape, BF16),
            pltpu.VMEM((1, LANES), F32),
            pltpu.VMEM((screening.shape[0], LANES), F32),
            pltpu.VMEM(vectors.shape, BF16),
            pltpu.SMEM(energies.shape, F32),
            pltpu.SMEM(k_coords.shape, jnp.int32),
            pltpu.VMEM((rows, 32, LANES), BF16),
            pltpu.VMEM((2, unit, LANES), F32),
            dma((8,)),
            pltpu.VMEM((cols, rows, 32, LANES), BF16),
            pltpu.VMEM((rows, nk, nb, LANES), BF16),
            pltpu.VMEM((batch, rows * 16), BF16),
            pltpu.VMEM((batch, rows * 16), BF16),
            pltpu.VMEM((LANES, nc * LANES), BF16),
            pltpu.VMEM((batch, kb * nvec), BF16),
            pltpu.VMEM((batch, batch), BF16),
            pltpu.VMEM((2 * points, count * 8), BF16),
            pltpu.VMEM((2 * LANES, LANES), BF16),
            pltpu.VMEM((cols, batch, LANES), BF16),
            pltpu.VMEM((cols, batch, LANES), F32),
            pltpu.VMEM((points, nvec, LANES), F32),
            pltpu.VMEM((cols, rows * 8, LANES), BF16),
            pltpu.VMEM((kb, points, LANES), F32),
            pltpu.VMEM((cols, nvec, LANES), F32),
            pltpu.VMEM((nc, rows, unit, nvec), F32),
            pltpu.VMEM((rows, unit, LANES), F32),
            pltpu.VMEM((rows, unit, LANES), F32),
            pltpu.VMEM((count, nvec // nc, LANES), F32),
            dma((cols, rows)), dma((cols, rows)),
            dma((rows,)), dma((rows,)),
            dma((cols,)), dma((cols,)),
            dma((count,)), dma((count,)),
            dma((rows,)), dma((rows,)),
        ],
        compiler_params=pltpu.CompilerParams(collective_id=0, has_side_effects=True),
    )(pair_exchange, conduction, valence, coulomb.reshape(1, planes), screening, vectors, energies, k_coords)


highest = lax.Precision.HIGHEST


def pair_factors(conduction, valence):
    count, valence_count, plane_count = valence.shape
    joined = (
        valence.astype(jnp.float32)[:, :, None, :] * conduction.astype(jnp.float32)[:, None, :, :]
    )
    return joined.reshape(count, valence_count * conduction.shape[1], plane_count).astype(
        jnp.bfloat16
    )


def transfer_index(rows_at, cols_at, mesh_cols):
    delta_first = jnp.mod(rows_at[:, None, 0] - cols_at[None, :, 0], MX)
    delta_second = jnp.mod(rows_at[:, None, 1] - cols_at[None, :, 1], mesh_cols)
    fold_first = jnp.minimum(delta_first, MX - delta_first)
    fold_second = jnp.minimum(delta_second, mesh_cols - delta_second)
    return (fold_first * (mesh_cols // 2 + 1) + fold_second).astype(jnp.int32)


def on_device(pair_exchange, conduction, valence, coulomb, screening, energies, vectors, k_coords):
    local_count, band_count, plane_count = pair_exchange.shape
    vector_count = vectors.shape[1] // band_count
    row_count = lax.axis_size("row")
    col_count = lax.axis_size("col")
    total_count = local_count * row_count * col_count
    mesh_cols = total_count // MX
    moving = vectors.reshape(local_count, band_count, vector_count)
    partial_density = jnp.einsum(
        "ktg,ktn->gn", pair_exchange, moving, preferred_element_type=jnp.float32
    )
    density = lax.psum(partial_density, ("row", "col"))
    block_size = 128
    sweeps = plane_count // block_size
    col_cond, col_val, col_vec, col_at = (
        lax.all_gather(conduction, "row", axis=0, tiled=True),
        lax.all_gather(valence, "row", axis=0, tiled=True),
        lax.all_gather(vectors, "row", axis=0, tiled=True),
        lax.all_gather(k_coords, "row", axis=0, tiled=True),
    )
    row_cond, row_val, row_at = (
        lax.all_gather(conduction, "col", axis=0, tiled=True),
        lax.all_gather(valence, "col", axis=0, tiled=True),
        lax.all_gather(k_coords, "col", axis=0, tiled=True),
    )
    row_pairs = pair_factors(row_cond, row_val)
    col_pairs = pair_factors(col_cond, col_val)
    indices = transfer_index(row_at, col_at, mesh_cols)
    col_moving = col_vec.reshape(-1, band_count, vector_count)

    def square_sweep(sweep_index, running):
        anchor = sweep_index * block_size
        coupling = jnp.take(
            lax.dynamic_slice_in_dim(screening, anchor, block_size, 1), indices, axis=0
        )
        row_block = lax.dynamic_slice_in_dim(row_pairs, anchor, block_size, 2)
        col_block = lax.dynamic_slice_in_dim(col_pairs, anchor, block_size, 2)
        col_proj = jnp.einsum(
            "ktg,ktn->kng", col_block, col_moving, preferred_element_type=jnp.float32
        )
        potential = jnp.einsum("ijg,jng->ing", coupling, col_proj, precision=highest)
        return running + jnp.einsum(
            "ktg,kng->ktn", row_block.astype(jnp.float32), potential, precision=highest
        )

    forward = lax.fori_loop(
        0,
        sweeps,
        square_sweep,
        jnp.zeros((row_pairs.shape[0], band_count, vector_count), jnp.float32),
    )
    owned = lax.psum_scatter(
        forward.reshape(col_count, local_count, band_count, vector_count),
        "col",
        scatter_dimension=0,
        tiled=True,
    )[0]
    moving_wide = moving.astype(jnp.float32)
    exchange_term = jnp.einsum(
        "ktg,gn->ktn", pair_exchange.astype(jnp.float32) * coulomb, density, precision=highest
    )
    applied = (
        energies[:, :, None] * moving_wide
        + 2.0 / (total_count * band_count) * exchange_term
        - owned / total_count
    )
    gram = jnp.einsum("ktm,ktn->mn", moving_wide, applied, precision=highest)
    alpha = lax.psum(gram, ("row", "col")) / (total_count * band_count)
    residual = applied - jnp.einsum("ktm,mn->ktn", moving_wide, alpha, precision=highest)
    return (residual.reshape(local_count, band_count * vector_count), alpha)


def fits(args, mesh):
    pair_exchange, conduction, valence, _, screening, _, vectors, _ = args
    rows, cols = mesh.shape["row"], mesh.shape["col"]
    points, nb, planes = pair_exchange.shape
    nk = points // (rows * cols)
    nv, nc = valence.shape[1], conduction.shape[1]
    nvec = vectors.shape[1] // nb
    return (
        planes == rows * LANES and nc * nvec == LANES and nk * nv == 8 and nk * (nv + nc) == 16
        and nk == 2 and nvec // nc == 8 and rows % 2 == 0 and cols % 2 == 0 and screening.shape[0] <= LANES
        and points <= LANES
    )


def solution(mesh):
    in_specs = (
        P(("row", "col"), None, None),
        P(("row", "col"), None, None),
        P(("row", "col"), None, None),
        P(),
        P(),
        P(("row", "col"), None),
        P(("row", "col"), None),
        P(("row", "col"), None),
    )
    out_specs = (P(("row", "col"), None), P())

    def run(*args):
        body = fast_on_device if fits(args, mesh) else on_device
        return jax.shard_map(
            body, mesh=mesh, in_specs=in_specs, out_specs=out_specs, check_vma=False
        )(*args)

    return run
```

profile of v0, /device:TPU:0, one launch (start us, length us, event | category | flops | bytes accessed | tf_op | source)
XLA Modules:
  0.0 27.2 jit_solution(8345826170451266519)
XLA Ops:
  0.6 25.3 %shard_map.95 = (f32[2,512]{1,0:T(2,128)S(1)}, f32[32,32]{1,0:T(8,128)S(1)}) custom-call(bf16[2,16,1024]{2,1,0:T(8,128)(2,1)} %px_hbm.1, bf16[2,4,1024]{2,1,0:T(4,128)(2,1)} %cond_hbm.1, bf16[2,4,1024]{2,1,0:T(4,128)(2,1)} %val_hbm.1, f32[1,1024]{1,0:T(1,128)} %bitcast.1, f32[34,1024]{1,0:T(8,128)} %screening_hbm.1, bf16[2,512]{1,0:T(2,128)(2,1)} %vec_hbm.1, ...), custom_call_target="tpu_custom_call" | custom-call | tf_op jit(solution)/shard_map/pallas_call | solution.py:357
  26.0 0.6 %copy.12 = f32[2,512]{1,0:T(2,128)} copy(f32[2,512]{1,0:T(2,128)S(1)} %get-tuple-element.2) | data formatting | bytes 8192
  26.6 0.6 %copy.13 = f32[32,32]{1,0:T(8,128)} copy(f32[32,32]{1,0:T(8,128)S(1)} %get-tuple-element.3) | data formatting | bytes 8192
where the time goes:
time: 27.4 us; the launch traced here: 27.2 us
  Pallas kernels  25.3 us (92%)
  local copies, waits for them, and re-layouts  1.2 us (4%)
  between operations  0.64 us (2%)
    pallas_call x1, Pallas kernels, fast_on_device(): pl.pallas_call(functools.partial(kernel, (rows, cols, nk, nv, nc, nvec, t...  25.3 us
    unnamed x2, local copies, waits for them, and re-layouts  1.2 us

commit v1 on v0

--- a/solution.py
+++ b/solution.py
@@ -37,7 +37,7 @@
     px_ref, cond_ref, val_ref, coulomb_ref, screening_ref, vec_ref, energy_ref, place_ref, msg_ref, wide_ref, load_sem,
     slots, px_slots, sel_v, sel_c, tile_m, block_m, perm, sel_k, screen, tiled, pairs, proj, coords, coupling,
     dens_slots, partial, out_send, out_slots, gram_slots,
-    in_send, in_recv, px_send, px_recv, dens_send, dens_recv, gram_send, gram_recv, o_send, o_recv,
+    in_recv, relay_recv, sends, arrivals,
 ):
     rows, cols, nk, nv, nc, nvec, total, mesh_cols = dims
     row, col = lax.axis_index("row"), lax.axis_index("col")
@@ -93,6 +93,72 @@
         msg_ref[r, 0:16] = message[:, r * LANES:(r + 1) * LANES]
         msg_ref[r, 16:32] = extra
 
+    loads[5].wait()
+    slots[col, row] = msg_ref[row]
+
+    pl.semaphore_wait(barrier, rows + cols - 2)
+
+    def in_copy(step):
+        pr = lax.rem(row + step, rows)
+        return pltpu.make_async_remote_copy(
+            src_ref=msg_ref.at[pr, 0:28], dst_ref=slots.at[col, row, 0:28],
+            send_sem=sends.at[0], recv_sem=in_recv.at[row],
+            device_id=(pr, col), device_id_type=MESH)
+
+    def across(step):
+        far = lax.rem(col // 2 + step // 2, cols // 2)
+        return far * 2 + lax.rem(lax.rem(col, 2) + lax.rem(step, 2), 2)
+
+    def relay_copy(r, step):
+        pc = across(step)
+        return pltpu.make_async_remote_copy(
+            src_ref=slots.at[col, r, 0:28], dst_ref=slots.at[col, r, 0:28],
+            send_sem=sends.at[1], recv_sem=relay_recv.at[col],
+            device_id=(row, pc), device_id_type=MESH)
+
+    def px_copy(step):
+        pr = lax.rem(row + step, rows)
+        return pltpu.make_async_remote_copy(
+            src_ref=px_ref.at[:, :, pl.ds(pl.multiple_of(pr * LANES, LANES), LANES)], dst_ref=px_slots.at[row],
+            send_sem=sends.at[2], recv_sem=arrivals.at[0],
+            device_id=(pr, col), device_id_type=MESH)
+
+    def dens_copy(step):
+        pc = lax.rem(col + step, cols)
+        return pltpu.make_async_remote_copy(
+            src_ref=dens_slots.at[col], dst_ref=dens_slots.at[col],
+            send_sem=sends.at[3], recv_sem=arrivals.at[1],
+            device_id=(row, pc), device_id_type=MESH)
+
+    def gram_copy(step):
+        pr, pc = other(step)
+        return pltpu.make_async_remote_copy(
+            src_ref=gram_slots.at[me], dst_ref=gram_slots.at[me],
+            send_sem=sends.at[4], recv_sem=arrivals.at[2],
+            device_id=(pr, pc), device_id_type=MESH)
+
+    def o_copy(step):
+        pr = lax.rem(row + step, rows)
+        return pltpu.make_async_remote_copy(
+            src_ref=out_send.at[pr], dst_ref=out_slots.at[row],
+            send_sem=sends.at[5], recv_sem=arrivals.at[3],
+            device_id=(pr, col), device_id_type=MESH)
+
+    def start_all(copy, end):
+        def body(step, carry):
+            copy(step).start()
+            return carry
+        lax.fori_loop(1, end, body, 0)
+
+    def landed(ref, sem):
+        pltpu.make_async_copy(ref, ref, sem).wait()
+
+    start_all(in_copy, rows)
+    start_all(px_copy, rows)
+    px_slots[row] = px_ref[:, :, mine]
+
+    for step in range(1, cols):
+        relay_copy(row, step).start()
     at = iota((batch, rows * 16), 0)
     to = iota((batch, rows * 16), 1)
     base = (at // unit) % rows * 16 + (at // nv) % nk * 8
@@ -111,84 +177,20 @@
     to = iota((2 * cols * kb, count * 8), 1)
     point = at % (cols * kb)
     sel_k[...] = one_hot(to == point // nk * 8 + at // (cols * kb) * nk + point % nk)
-    for load in loads[5:]:
+    for load in loads[6:]:
         load.wait()
-    slots[col, row] = msg_ref[row]
     high, low = split_pair(jnp.concatenate(
         [screening_ref[...], jnp.zeros((LANES - screening_ref.shape[0], LANES), F32)], axis=0))
     screen[0:LANES] = high
     screen[LANES:2 * LANES] = low
 
-    pl.semaphore_wait(barrier, rows + cols - 2)
-
-    def in_copy(step):
-        pr = lax.rem(row + step, rows)
-        return pltpu.make_async_remote_copy(
-            src_ref=msg_ref.at[pr, 0:28], dst_ref=slots.at[col, row, 0:28],
-            send_sem=in_send.at[col, pr], recv_sem=in_recv.at[col, row],
-            device_id=(pr, col), device_id_type=MESH)
-
-    def across(step):
-        far = lax.rem(col // 2 + step // 2, cols // 2)
-        return far * 2 + lax.rem(lax.rem(col, 2) + lax.rem(step, 2), 2)
-
-    def relay_copy(r, step):
-        pc = across(step)
-        return pltpu.make_async_remote_copy(
-            src_ref=slots.at[col, r, 0:28], dst_ref=slots.at[col, r, 0:28],
-            send_sem=in_send.at[pc, r], recv_sem=in_recv.at[col, r],
-            device_id=(row, pc), device_id_type=MESH)
-
-    def px_copy(step):
-        pr = lax.rem(row + step, rows)
-        return pltpu.make_async_remote_copy(
-            src_ref=px_ref.at[:, :, pl.ds(pl.multiple_of(pr * LANES, LANES), LANES)], dst_ref=px_slots.at[row],
-            send_sem=px_send.at[pr], recv_sem=px_recv.at[row],
-            device_id=(pr, col), device_id_type=MESH)
-
-    def dens_copy(step):
-        pc = lax.rem(col + step, cols)
-        return pltpu.make_async_remote_copy(
-            src_ref=dens_slots.at[col], dst_ref=dens_slots.at[col],
-            send_sem=dens_send.at[pc], recv_sem=dens_recv.at[col],
-            device_id=(row, pc), device_id_type=MESH)
-
-    def gram_copy(step):
-        pr, pc = other(step)
-        return pltpu.make_async_remote_copy(
-            src_ref=gram_slots.at[me], dst_ref=gram_slots.at[me],
-            send_sem=gram_send.at[pr * cols + pc], recv_sem=gram_recv.at[me],
-            device_id=(pr, pc), device_id_type=MESH)
-
-    def o_copy(step):
-        pr = lax.rem(row + step, rows)
-        return pltpu.make_async_remote_copy(
-            src_ref=out_send.at[pr], dst_ref=out_slots.at[row],
-            send_sem=o_send.at[pr], recv_sem=o_recv.at[row],
-            device_id=(pr, col), device_id_type=MESH)
-
-    def start_all(copy, end):
-        def body(step, carry):
-            copy(step).start()
-            return carry
-        lax.fori_loop(1, end, body, 0)
-
-    def landed(ref, sem):
-        pltpu.make_async_copy(ref, ref, sem).wait()
-
-    start_all(in_copy, rows)
-    start_all(px_copy, rows)
-    px_slots[row] = px_ref[:, :, mine]
-
     def relay(d, carry):
         r = lax.rem(row + d, rows)
-        landed(slots.at[col, r, 0:28], in_recv.at[col, r])
+        landed(slots.at[col, r, 0:28], in_recv.at[r])
         for step in range(1, cols):
             relay_copy(r, step).start()
         return carry
 
-    for step in range(1, cols):
-        relay_copy(row, step).start()
     lax.fori_loop(1, rows, relay, 0)
 
     def take_batch(which):
@@ -209,12 +211,7 @@
 
     take_batch(col)
 
-    def px_wait(step, carry):
-        r = lax.rem(row + step, rows)
-        landed(px_slots.at[r], px_recv.at[r])
-        return carry
-
-    lax.fori_loop(1, rows, px_wait, 0)
+    landed(px_slots.at[0:rows - 1], arrivals.at[0])
     px = dot(perm[...], px_slots[...].reshape(rows * nk * nb, LANES), (1, 0)).astype(BF16)
     own_x = tiled[col][:, 0:nvec]
     dens_slots[col] = dot(own_x, px, (0, 0))
@@ -222,12 +219,7 @@
 
     def rest_batches(step, carry):
         c = across(step)
-
-        def wait_one(r, inner):
-            landed(slots.at[c, r, 0:28], in_recv.at[c, r])
-            return inner
-
-        lax.fori_loop(0, rows, wait_one, 0)
+        landed(slots.at[c, :, 0:28], relay_recv.at[c])
         take_batch(c)
         return carry
 
@@ -251,12 +243,7 @@
     for i in range(kb):
         coupling[i] = dot(jnp.concatenate([hots[i], hots[i]], axis=1), screen[...], (1, 0))
 
-    def dens_wait(step, carry):
-        c = lax.rem(col + step, cols)
-        landed(dens_slots.at[c], dens_recv.at[c])
-        return carry
-
-    lax.fori_loop(1, cols, dens_wait, 0)
+    landed(dens_slots.at[0:cols - 1], arrivals.at[1])
     density = dens_slots[0]
     for c in range(1, cols):
         density = density + dens_slots[c]
@@ -296,19 +283,10 @@
     gram_slots[me] = jnp.concatenate([gram[s * step:(s + 1) * step] for s in range(nc)], axis=1)
     start_all(gram_copy, count)
 
-    def o_wait(d, acc):
-        r = lax.rem(row + d, rows)
-        landed(out_slots.at[r], o_recv.at[r])
-        return acc + out_slots[r]
-
-    applied = lax.fori_loop(1, rows, o_wait, out_send[row])
-
-    def gram_wait(d, carry):
-        p = lax.rem(me + d, count)
-        landed(gram_slots.at[p], gram_recv.at[p])
-        return carry
-
-    lax.fori_loop(1, count, gram_wait, 0)
+    out_slots[row] = out_send[row]
+    landed(out_slots.at[0:rows - 1], arrivals.at[3])
+    applied = jnp.sum(out_slots[...], axis=0)
+    landed(gram_slots.at[0:count - 1], arrivals.at[2])
     sums = jnp.sum(gram_slots[...], axis=0) * (1.0 / (total * nb))
     alpha = jnp.concatenate([sums[:, s * nvec:(s + 1) * nvec] for s in range(nc)], axis=0)
     alpha_ref[...] = alpha
@@ -321,24 +299,12 @@
         out_ref[:, j * LANES:(j + 1) * LANES] = jnp.concatenate(
             [residual[k * nv + j:k * nv + j + 1] for k in range(nk)], axis=0)
 
-    def drain(copy, end):
-        def body(d, carry):
-            copy(d).wait_send()
-            return carry
-        lax.fori_loop(1, end, body, 0)
-
-    drain(in_copy, rows)
-
-    def drain_relay(r, carry):
-        for step in range(1, cols):
-            relay_copy(r, step).wait_send()
-        return carry
-
-    lax.fori_loop(0, rows, drain_relay, 0)
-    drain(px_copy, rows)
-    drain(dens_copy, cols)
-    drain(o_copy, rows)
-    drain(gram_copy, count)
+    landed(slots.at[0, 0:rows - 1, 0:28], sends.at[0])
+    landed(slots.at[0:cols - 1, :, 0:28], sends.at[1])
+    landed(px_slots.at[0:rows - 1], sends.at[2])
+    landed(dens_slots.at[0:cols - 1], sends.at[3])
+    landed(gram_slots.at[0:count - 1], sends.at[4])
+    landed(out_slots.at[0:rows - 1], sends.at[5])
 
 
 def fast_on_device(pair_exchange, conduction, valence, coulomb, screening, energies, vectors, k_coords):
@@ -393,11 +359,7 @@
             pltpu.VMEM((rows, unit, LANES), F32),
             pltpu.VMEM((rows, unit, LANES), F32),
             pltpu.VMEM((count, nvec // nc, LANES), F32),
-            dma((cols, rows)), dma((cols, rows)),
-            dma((rows,)), dma((rows,)),
-            dma((cols,)), dma((cols,)),
-            dma((count,)), dma((count,)),
-            dma((rows,)), dma((rows,)),
+            dma((rows,)), dma((cols,)), dma((6,)), dma((4,)),
         ],
         compiler_params=pltpu.CompilerParams(collective_id=0, has_side_effects=True),
     )(pair_exchange, conduction, valence, coulomb.reshape(1, planes), screening, vectors, energies, k_coords)

time: 27.4 us -> 25.1 us (0.916)
  Pallas kernels: 25.3 us -> 23 us
    pallas_call x1, Pallas kernels: 25.3 us -> 23 us  [fast_on_device(): pl.pallas_call(functools.partial(kernel, (rows, cols, nk, nv, nc, nvec, t...]
where the time goes in v1:
time: 25.1 us; the launch traced here: 24.8 us
  Pallas kernels  23 us (92%)
  local copies, waits for them, and re-layouts  1.2 us (5%)
  between operations  0.64 us (3%)
    pallas_call x1, Pallas kernels, fast_on_device(): pl.pallas_call(functools.partial(kernel, (rows, cols, nk, nv, nc, nvec, t...  23 us
    unnamed x2, local copies, waits for them, and re-layouts  1.2 us

profile of v1, /device:TPU:0, one launch (start us, length us, event | category | flops | bytes accessed | tf_op | source)
XLA Modules:
  0.0 24.8 jit_solution(14754416595546252172)
XLA Ops:
  0.6 23.0 %shard_map.95 = (f32[2,512]{1,0:T(2,128)S(1)}, f32[32,32]{1,0:T(8,128)S(1)}) custom-call(bf16[2,16,1024]{2,1,0:T(8,128)(2,1)} %px_hbm.1, bf16[2,4,1024]{2,1,0:T(4,128)(2,1)} %cond_hbm.1, bf16[2,4,1024]{2,1,0:T(4,128)(2,1)} %val_hbm.1, f32[1,1024]{1,0:T(1,128)} %bitcast.1, f32[34,1024]{1,0:T(8,128)} %screening_hbm.1, bf16[2,512]{1,0:T(2,128)(2,1)} %vec_hbm.1, ...), custom_call_target="tpu_custom_call" | custom-call | tf_op jit(solution)/shard_map/pallas_call | solution.py:323
  23.6 0.6 %copy.12 = f32[2,512]{1,0:T(2,128)} copy(f32[2,512]{1,0:T(2,128)S(1)} %get-tuple-element.2) | data formatting | bytes 8192
  24.2 0.6 %copy.13 = f32[32,32]{1,0:T(8,128)} copy(f32[32,32]{1,0:T(8,128)S(1)} %get-tuple-element.3) | data formatting | bytes 8192

commit v2 on v1

v2 whole, which is shorter than its diff:
```python
import functools
import math

import jax
import jax.numpy as jnp
from jax import lax
from jax.experimental import pallas as pl
from jax.experimental.pallas import tpu as pltpu
from jax.sharding import PartitionSpec as P

MX = 32
LANES = 128
MESH = pl.DeviceIdType.MESH
F32 = jnp.float32
BF16 = jnp.bfloat16


def split_pair(value):
    high = value.astype(BF16)
    return high, (value - high.astype(F32)).astype(BF16)


def dot(a, b, contract):
    return lax.dot_general(a, b, ((contract[0:1], contract[1:2]), ((), ())), preferred_element_type=F32)


def iota(shape, axis):
    return lax.broadcasted_iota(jnp.int32, shape, axis)


def one_hot(condition):
    return jnp.where(condition, 1.0, 0.0).astype(BF16)


def wide_dot(a, b, contract):
    high, low = a
    main, rest = b
    return dot(high, main, contract) + dot(low, main, contract) + dot(high, rest, contract)


def swap_blocks(tile, lanes, rows):
    row_bit = (iota(tile.shape, 0) // rows) % 2
    lane_bit = (iota(tile.shape, 1) // lanes) % 2
    up = pltpu.roll(pltpu.roll(tile, lanes, 1), tile.shape[0] - rows, 0)
    down = pltpu.roll(pltpu.roll(tile, LANES - lanes, 1), rows, 0)
    return jnp.where(row_bit == lane_bit, tile, jnp.where(lane_bit == 1, up, down))


def fold_blocks(square, width):
    kept = jnp.where(iota(square.shape, 0) // width == iota(square.shape, 1) // width, square, 0.0)
    rows = kept[0:width]
    for at in range(width, square.shape[0], width):
        rows = rows + kept[at:at + width]
    half = rows + pltpu.roll(rows, LANES // 2, 1)
    return half + pltpu.roll(half, LANES // 4, 1)


def basis(phase, sign):
    angle = (phase % MX).astype(F32) * (2.0 * math.pi / MX)
    return (jnp.cos(angle) + jnp.sin(angle)) * (1 - 2 * (sign % 2)).astype(F32)


def kernel(
    dims, px_hbm, cond_hbm, val_hbm, coulomb_hbm, screening_hbm, vec_hbm, energy_hbm, place_hbm,
    out_ref, alpha_ref,
    px_ref, cond_ref, val_ref, coulomb_ref, screening_ref, vec_ref, energy_ref, place_ref,
    load_sem, msg_ref, slots, px_msg, px_slots, select, select_q, lam, pairs, moved, proj, part, out_send, out_slots, gram_slots,
    sends, arrivals,
):
    rows, cols, nk, nv, nc, nvec, total = dims
    row, col = lax.axis_index("row"), lax.axis_index("col")
    me = row * cols + col
    count = rows * cols
    nb = nv * nc
    width = LANES // cols
    deep = width // 2
    unit = nk * nv
    half = LANES // 2

    depth, core = row // 2, lax.rem(row, 2)
    back, odd = depth // 2, lax.rem(depth, 2)
    layers = [3 * (1 - back), 2 - back, depth + 1 - 2 * odd, depth]
    far_rows = [2 * layer + side for layer in layers for side in (1 - core, core)]
    left = lax.rem(col, 2)
    far_cols = [cols - 1 - col, lax.rem(col + 2, cols), col + 1 - 2 * left, col]
    peers = [(pr, pc) for i, pr in enumerate(far_rows) for j, pc in enumerate(far_cols) if i + j + 2 < rows + cols]
    mixed_peers = [(pr, pc) for j, pc in enumerate(far_cols) for i, pr in enumerate(far_rows) if i + j + 2 < rows + cols]
    ring_rows = [row] + [lax.rem(row + step, rows) for step in range(1, rows)]
    ring_cols = [col] + [lax.rem(col + step, cols) for step in range(1, cols)]
    ring_peers = [(pr, pc) for i, pr in enumerate(ring_rows) for j, pc in enumerate(ring_cols) if i + j]
    ring2_peers = [(pr, pc) for j, pc in enumerate(ring_cols) for i, pr in enumerate(ring_rows) if i + j]
    near_peers = peers[::-1]
    barrier = pltpu.get_barrier_semaphore()
    for peer in peers:
        pl.semaphore_signal(barrier, inc=1, device_id=peer, device_id_type=MESH)

    mine = pl.ds(pl.multiple_of(row * LANES, LANES), LANES)
    loads = [
        pltpu.make_async_copy(src, dst, load_sem.at[at])
        for at, (src, dst) in enumerate((
            (val_hbm, val_ref), (cond_hbm, cond_ref), (vec_hbm, vec_ref), (place_hbm, place_ref), (px_hbm, px_ref),
            (energy_hbm, energy_ref), (screening_hbm.at[:, mine], screening_ref), (coulomb_hbm.at[:, mine], coulomb_ref)))
    ]
    for load in loads:
        load.start()
    row8 = iota((8, LANES), 0)
    lane8 = iota((8, LANES), 1)
    slots[:, 14:16] = jnp.zeros((count, 2, LANES), BF16)
    px_slots[:, 8:16] = jnp.zeros((count, 8, LANES), BF16)
    for load in loads[:4]:
        load.wait()

    vec = vec_ref[...].astype(F32)
    own = jnp.concatenate(
        [vec[k:k + 1, j * LANES:(j + 1) * LANES] for k in range(nk) for j in range(nv)], axis=0)
    tail = jnp.zeros((8, LANES), F32)
    wave = lane8 % half
    for k in range(nk):
        value = basis((wave // 2) * place_ref[k, 0], (wave % 2) * place_ref[k, 1])
        high = value.astype(BF16).astype(F32)
        tail = jnp.where(row8 == 2 * nk + k, jnp.where(lane8 < half, high, value - high), tail)
    for r in range(rows):
        span = slice(r * LANES, (r + 1) * LANES)
        turned = []
        for k in range(nk):
            tile = jnp.concatenate([val_ref[k, :, span].astype(F32), cond_ref[k, :, span].astype(F32)], axis=0)
            for size in (4, 2, 1):
                tile = swap_blocks(tile, deep * size, size)
            turned.append(tile)
        for q in range(cols):
            low = tail
            for k in range(nk):
                shift = (2 * k - 2 * q) % 8
                piece = turned[k] if shift == 0 else pltpu.roll(turned[k], shift, 0)
                low = jnp.where(row8 // 2 == k, piece, low)
            msg_ref[r * cols + q] = jnp.concatenate([own, low], axis=0).astype(BF16)

    pl.semaphore_wait(barrier, count - 1)

    def main_copy(device):
        peer = device[0] * cols + device[1]
        return pltpu.make_async_remote_copy(
            src_ref=msg_ref.at[peer, 0:14], dst_ref=slots.at[me, 0:14],
            send_sem=sends.at[0], recv_sem=arrivals.at[0], device_id=device, device_id_type=MESH)

    def px_copy(device):
        peer = device[0] * cols + device[1]
        return pltpu.make_async_remote_copy(
            src_ref=px_msg.at[peer], dst_ref=px_slots.at[me, 0:8],
            send_sem=sends.at[1], recv_sem=arrivals.at[1], device_id=device, device_id_type=MESH)

    def out_copy(device):
        peer = device[0] * cols + device[1]
        return pltpu.make_async_remote_copy(
            src_ref=out_send.at[peer], dst_ref=out_slots.at[me],
            send_sem=sends.at[2], recv_sem=arrivals.at[2], device_id=device, device_id_type=MESH)

    def gram_copy(device):
        return pltpu.make_async_remote_copy(
            src_ref=gram_slots.at[me], dst_ref=gram_slots.at[me],
            send_sem=sends.at[3], recv_sem=arrivals.at[3], device_id=device, device_id_type=MESH)

    def start_all(copy, targets):
        for peer in targets:
            copy(peer).start()

    def pack(block):
        piece = block[0:8]
        for b in range(1, nc):
            piece = jnp.where(lane8 // nvec == b, block[b * 8:b * 8 + 8], piece)
        return piece

    def landed(ref, sem):
        pltpu.make_async_copy(ref, ref, sem).wait()

    start_all(main_copy, mixed_peers)
    slots[me] = msg_ref[me]

    loads[4].wait()
    at = iota((nk * nb, nk * nb), 0)
    to = iota((nk * nb, nk * nb), 1)
    order = one_hot(to == (at % unit) // nv * nb + at % nv * nc + at // unit)
    arranged = dot(order, px_ref[...].reshape(nk * nb, px_ref.shape[2]), (1, 0))
    for r in range(rows):
        span = slice(r * LANES, (r + 1) * LANES)
        for q in range(cols):
            tile = arranged[q * 8:q * 8 + 8, span]
            for b in range(cols):
                if b != q:
                    moving = pltpu.roll(arranged[b * 8:b * 8 + 8, span], (width * (b - q)) % LANES, 1)
                    tile = jnp.where(lane8 // width == b, moving, tile)
            px_msg[r * cols + q] = tile.astype(BF16)
    start_all(px_copy, mixed_peers)
    px_slots[me, 0:8] = px_msg[me]

    at = iota((count * 16, LANES), 0)
    to = iota((count * 16, LANES), 1)
    same = at // 16 == (to % half) // nk
    place = at % 16
    select[:, 0:LANES] = one_hot(same & (place == 8 + to % nk * 2 + to // half))
    for j in range(nv):
        select[:, (j + 1) * LANES:(j + 2) * LANES] = one_hot(same & (place == to % nk * nv + j))
    at = iota((LANES, count * 16), 0)
    to = iota((LANES, count * 16), 1)
    select_q[...] = one_hot((to // 16 == (at % half) // nk) & (to % 16 == 12 + at % nk))
    for load in loads[5:]:
        load.wait()
    at = iota((LANES, LANES), 0)
    to = iota((LANES, LANES), 1)
    fold = at // 2
    angle = ((fold * ((to % half) // 2)) % MX).astype(F32) * (2.0 * math.pi / MX)
    weight = jnp.where((fold == 0) | (fold == MX // 2), 1.0, 2.0) * (1 - 2 * ((at % 2) * (to % 2))).astype(F32)
    table = jnp.where(fold <= MX // 2, jnp.cos(angle) * weight, 0.0)
    screened = jnp.concatenate(
        [screening_ref[...], jnp.zeros((LANES - screening_ref.shape[0], LANES), F32)], axis=0)
    lam[...] = wide_dot(split_pair(screened), split_pair(table), (0, 0)) * (-1.0 / (total * total))
    band = lam[pl.ds(pl.multiple_of(col * width, 8), width), :]
    spectrum = jnp.where(iota((deep, LANES), 1) < half, band[0:deep], band[deep:width])
    charge = jnp.broadcast_to(coulomb_ref[...], (width, LANES))
    lane_w = iota((width, LANES), 1)
    tiles = jnp.zeros((width, LANES), F32)
    for b in range(cols):
        for q in range(cols):
            moving = charge if b == q else pltpu.roll(charge, (width * (b - q)) % LANES, 1)
            tiles = jnp.where((lane_w // width == b) & (col == q), moving, tiles)
    charge = tiles * (2.0 / (total * nb))
    energy = jnp.zeros((8, LANES), F32)
    for k in range(nk):
        for t in range(nb):
            energy = jnp.where((row8 == k * nv + t // nc) & (lane8 // nvec == t % nc), energy_ref[k, t], energy)

    lifted = energy * own
    high, low = split_pair(lifted)
    own_low = own.astype(BF16)
    base = pack(fold_blocks(dot(own_low, high, (0, 0)) + dot(own_low, low, (0, 0)), nvec))

    landed(slots.at[0:count - 1, 0:14], arrivals.at[0])
    everything = slots[...].reshape(count * 16, LANES)
    spread = dot(everything, select[...], (0, 0))
    for v in range(nv):
        for c in range(nc):
            joined = spread[v * deep:(v + 1) * deep, 0:LANES] * spread[half + c * deep:half + (c + 1) * deep, 0:LANES]
            pairs[v * nc + c] = joined.astype(BF16).astype(F32)
    for t in range(nb):
        moved[t] = spread[t % nc * nvec:(t % nc + 1) * nvec, (t // nc + 1) * LANES:(t // nc + 2) * LANES]
    waves = dot(select_q[...], everything, (1, 0))
    crossed = pltpu.roll(waves, half, 1)
    first = (at < half) & (to < half)
    second = (at >= half) & (to >= half)
    waves = (
        jnp.where(first, waves, jnp.where(second, crossed, 0.0)).astype(BF16),
        jnp.where(first, crossed, jnp.where(second, waves, 0.0)).astype(BF16))

    group = 2
    for first_l in range(0, deep, group):
        sums_l = [None] * group
        for t in range(nb):
            for u in range(group):
                term = pairs[t, first_l + u:first_l + u + 1, :] * moved[t]
                sums_l[u] = term if t == 0 else sums_l[u] + term
        for u in range(group):
            proj[first_l + u] = sums_l[u]
    spectral = wide_dot(split_pair(proj[...].reshape(deep * nvec, LANES)), waves, (1, 0)).reshape(deep, nvec, LANES)
    scaled = spectral * spectrum[:, None, :]
    sides = [
        split_pair(jnp.concatenate([side[l] for l in range(deep)], axis=1)) for side in (spectral, scaled)]
    gram = wide_dot(*sides, (1, 1))

    landed(px_slots.at[0:count - 1, 0:8], arrivals.at[1])
    exchange = px_slots[...].reshape(count * 16, LANES)
    density = fold_blocks(dot(everything, exchange, (0, 0)), nvec)
    charged = density * charge
    gram = gram + wide_dot(split_pair(density), split_pair(charged * (1.0 / cols)), (1, 1))
    gram = jnp.concatenate([gram] * nc, axis=1)
    gram_slots[me] = (base + pack(gram)).astype(BF16)
    start_all(gram_copy, ring_peers)

    proj[...] = wide_dot(
        split_pair(scaled.reshape(deep * nvec, LANES)), waves, (1, 1)).reshape(deep, nvec, LANES)
    lifted_x = jnp.where(
        at // nvec == to // width, jnp.concatenate([charged] * (LANES // nvec), axis=0), 0.0)
    high, low = split_pair(lifted_x)
    whole = dot(exchange, high, (1, 1)) + dot(exchange, low, (1, 1))
    for first_t in range(0, nb, group):
        sums_t = [None] * group
        for l in range(deep):
            for u in range(group):
                term = pairs[first_t + u, l:l + 1, :] * proj[l]
                sums_t[u] = term if l == 0 else sums_t[u] + term
        for u in range(group):
            moved[first_t + u] = sums_t[u]
    placed = jnp.concatenate(
        [jnp.concatenate([moved[j * nc + c] for c in range(nc)], axis=0) for j in range(nv)], axis=1)
    high, low = split_pair(placed)
    chosen = select[:, LANES:]
    whole = whole + dot(chosen, high, (1, 1)) + dot(chosen, low, (1, 1))
    part[...] = whole.reshape(count, 16, LANES)
    out_send[...] = part[:, 0:8].astype(BF16)
    start_all(out_copy, ring_peers)
    out_slots[me] = jnp.zeros((8, LANES), BF16)
    kept = part[me, 0:8] + lifted

    landed(gram_slots.at[0:count - 1], arrivals.at[3])
    sums = jnp.sum(gram_slots[...].astype(F32), axis=0) * (1.0 / (total * nb))
    turns = [sums] + [pltpu.roll(sums, b * nvec, 1) for b in range(1, nc)]
    for b in range(nc):
        alpha_ref[b * 8:b * 8 + 8] = turns[(-b) % nc][:, 0:nvec]
    mixed = jnp.concatenate(
        [jnp.where(lane8 // nvec == q, turns[(q - b) % nc], 0.0) for q in range(nc) for b in range(nc)], axis=0)
    high, low = split_pair(mixed)
    taken = dot(own_low, high, (1, 0)) + dot(own_low, low, (1, 0))

    landed(out_slots.at[0:count - 1], arrivals.at[2])
    residual = kept - taken + jnp.sum(out_slots[...].astype(F32), axis=0)
    for j in range(nv):
        out_ref[:, j * LANES:(j + 1) * LANES] = jnp.concatenate(
            [residual[k * nv + j:k * nv + j + 1] for k in range(nk)], axis=0)

    landed(slots.at[0:count - 1, 0:14], sends.at[0])
    landed(px_slots.at[0:count - 1, 0:8], sends.at[1])
    landed(out_slots.at[0:count - 1], sends.at[2])
    landed(gram_slots.at[0:count - 1], sends.at[3])


def finish(out_ref, alpha_ref, out_hbm, alpha_hbm, sems):
    copies = [
        pltpu.make_async_copy(src, dst, sems.at[at])
        for at, (src, dst) in enumerate(((out_ref, out_hbm), (alpha_ref, alpha_hbm)))]
    for copy in copies:
        copy.start()
    for copy in copies:
        copy.wait()


def fast_on_device(pair_exchange, conduction, valence, coulomb, screening, energies, vectors, k_coords):
    nk, nb, planes = pair_exchange.shape
    nv, nc = valence.shape[1], conduction.shape[1]
    nvec = vectors.shape[1] // nb
    rows, cols = lax.axis_size("row"), lax.axis_size("col")
    count = rows * cols
    total = nk * count
    deep = LANES // cols // 2
    vmem = pl.BlockSpec(memory_space=pltpu.VMEM)
    dma = pltpu.SemaphoreType.DMA
    results = pl.pallas_call(
        functools.partial(kernel, (rows, cols, nk, nv, nc, nvec, total)),
        out_shape=(
            pltpu.VMEM((nk, nb * nvec), F32),
            pltpu.VMEM((nvec, nvec), F32),
        ),
        in_specs=[pl.BlockSpec(memory_space=pl.ANY)] * 8,
        out_specs=(vmem, vmem),
        scratch_shapes=[
            pltpu.VMEM(pair_exchange.shape, BF16),
            pltpu.VMEM(conduction.shape, BF16),
            pltpu.VMEM(valence.shape, BF16),
            pltpu.VMEM((1, LANES), F32),
            pltpu.VMEM((screening.shape[0], LANES), F32),
            pltpu.VMEM(vectors.shape, BF16),
            pltpu.SMEM(energies.shape, F32),
            pltpu.SMEM(k_coords.shape, jnp.int32),
            dma((8,)),
            pltpu.VMEM((count, 16, LANES), BF16),
            pltpu.VMEM((count, 16, LANES), BF16),
            pltpu.VMEM((count, 8, LANES), BF16),
            pltpu.VMEM((count, 16, LANES), BF16),
            pltpu.VMEM((count * 16, (1 + nv) * LANES), BF16),
            pltpu.VMEM((LANES, count * 16), BF16),
            pltpu.VMEM((LANES, LANES), F32),
            pltpu.VMEM((nb, deep, LANES), F32),
            pltpu.VMEM((nb, nvec, LANES), F32),
            pltpu.VMEM((deep, nvec, LANES), F32),
            pltpu.VMEM((count, 16, LANES), F32),
            pltpu.VMEM((count, 8, LANES), BF16),
            pltpu.VMEM((count, 8, LANES), BF16),
            pltpu.VMEM((count, 8, LANES), BF16),
            dma((4,)), dma((4,)),
        ],
        compiler_params=pltpu.CompilerParams(collective_id=0, has_side_effects=True),
    )(pair_exchange, conduction, valence, coulomb.reshape(1, planes), screening, vectors, energies, k_coords)
    return pl.pallas_call(
        finish,
        out_shape=(jax.ShapeDtypeStruct((nk, nb * nvec), F32), jax.ShapeDtypeStruct((nvec, nvec), F32)),
        in_specs=[vmem, vmem],
        out_specs=(pl.BlockSpec(memory_space=pl.ANY), pl.BlockSpec(memory_space=pl.ANY)),
        scratch_shapes=[dma((2,))],
    )(*[pltpu.with_memory_space_constraint(result, pltpu.VMEM) for result in results])


highest = lax.Precision.HIGHEST


def pair_factors(conduction, valence):
    count, valence_count, plane_count = valence.shape
    joined = (
        valence.astype(jnp.float32)[:, :, None, :] * conduction.astype(jnp.float32)[:, None, :, :]
    )
    return joined.reshape(count, valence_count * conduction.shape[1], plane_count).astype(
        jnp.bfloat16
    )


def transfer_index(rows_at, cols_at, mesh_cols):
    delta_first = jnp.mod(rows_at[:, None, 0] - cols_at[None, :, 0], MX)
    delta_second = jnp.mod(rows_at[:, None, 1] - cols_at[None, :, 1], mesh_cols)
    fold_first = jnp.minimum(delta_first, MX - delta_first)
    fold_second = jnp.minimum(delta_second, mesh_cols - delta_second)
    return (fold_first * (mesh_cols // 2 + 1) + fold_second).astype(jnp.int32)


def on_device(pair_exchange, conduction, valence, coulomb, screening, energies, vectors, k_coords):
    local_count, band_count, plane_count = pair_exchange.shape
    vector_count = vectors.shape[1] // band_count
    row_count = lax.axis_size("row")
    col_count = lax.axis_size("col")
    total_count = local_count * row_count * col_count
    mesh_cols = total_count // MX
    moving = vectors.reshape(local_count, band_count, vector_count)
    partial_density = jnp.einsum(
        "ktg,ktn->gn", pair_exchange, moving, preferred_element_type=jnp.float32
    )
    density = lax.psum(partial_density, ("row", "col"))
    block_size = 128
    sweeps = plane_count // block_size
    col_cond, col_val, col_vec, col_at = (
        lax.all_gather(conduction, "row", axis=0, tiled=True),
        lax.all_gather(valence, "row", axis=0, tiled=True),
        lax.all_gather(vectors, "row", axis=0, tiled=True),
        lax.all_gather(k_coords, "row", axis=0, tiled=True),
    )
    row_cond, row_val, row_at = (
        lax.all_gather(conduction, "col", axis=0, tiled=True),
        lax.all_gather(valence, "col", axis=0, tiled=True),
        lax.all_gather(k_coords, "col", axis=0, tiled=True),
    )
    row_pairs = pair_factors(row_cond, row_val)
    col_pairs = pair_factors(col_cond, col_val)
    indices = transfer_index(row_at, col_at, mesh_cols)
    col_moving = col_vec.reshape(-1, band_count, vector_count)

    def square_sweep(sweep_index, running):
        anchor = sweep_index * block_size
        coupling = jnp.take(
            lax.dynamic_slice_in_dim(screening, anchor, block_size, 1), indices, axis=0
        )
        row_block = lax.dynamic_slice_in_dim(row_pairs, anchor, block_size, 2)
        col_block = lax.dynamic_slice_in_dim(col_pairs, anchor, block_size, 2)
        col_proj = jnp.einsum(
            "ktg,ktn->kng", col_block, col_moving, preferred_element_type=jnp.float32
        )
        potential = jnp.einsum("ijg,jng->ing", coupling, col_proj, precision=highest)
        return running + jnp.einsum(
            "ktg,kng->ktn", row_block.astype(jnp.float32), potential, precision=highest
        )

    forward = lax.fori_loop(
        0,
        sweeps,
        square_sweep,
        jnp.zeros((row_pairs.shape[0], band_count, vector_count), jnp.float32),
    )
    owned = lax.psum_scatter(
        forward.reshape(col_count, local_count, band_count, vector_count),
        "col",
        scatter_dimension=0,
        tiled=True,
    )[0]
    moving_wide = moving.astype(jnp.float32)
    exchange_term = jnp.einsum(
        "ktg,gn->ktn", pair_exchange.astype(jnp.float32) * coulomb, density, precision=highest
    )
    applied = (
        energies[:, :, None] * moving_wide
        + 2.0 / (total_count * band_count) * exchange_term
        - owned / total_count
    )
    gram = jnp.einsum("ktm,ktn->mn", moving_wide, applied, precision=highest)
    alpha = lax.psum(gram, ("row", "col")) / (total_count * band_count)
    residual = applied - jnp.einsum("ktm,mn->ktn", moving_wide, alpha, precision=highest)
    return (residual.reshape(local_count, band_count * vector_count), alpha)


def fits(args, mesh):
    pair_exchange, conduction, valence, _, screening, _, vectors, _ = args
    rows, cols = mesh.shape["row"], mesh.shape["col"]
    points, nb, planes = pair_exchange.shape
    nk = points // (rows * cols)
    nv, nc = valence.shape[1], conduction.shape[1]
    nvec = vectors.shape[1] // nb
    return (
        planes == rows * LANES and rows == 8 and cols == 4 and rows * cols * nk * 2 == LANES and nk == 2 and nv == 4 and nc == 4
        and nc * nvec == LANES and points == 2 * MX and screening.shape[0] == MX + 2
    )


def solution(mesh):
    in_specs = (
        P(("row", "col"), None, None),
        P(("row", "col"), None, None),
        P(("row", "col"), None, None),
        P(),
        P(),
        P(("row", "col"), None),
        P(("row", "col"), None),
        P(("row", "col"), None),
    )
    out_specs = (P(("row", "col"), None), P())

    def run(*args):
        body = fast_on_device if fits(args, mesh) else on_device
        return jax.shard_map(
            body, mesh=mesh, in_specs=in_specs, out_specs=out_specs, check_vma=False
        )(*args)

    return run
```

time: 25.1 us -> 20.8 us (0.83)
  Pallas kernels: 23 us -> 19.9 us
  local copies, waits for them, and re-layouts: 1.2 us -> 0 us
    pallas_call x1, Pallas kernels: 23 us -> 19.3 us  [fast_on_device(): pl.pallas_call(functools.partial(kernel, (rows, cols, nk, nv, nc, nvec, t...]
    unnamed x2 -> x0, local copies, waits for them, and re-layouts: 1.2 us -> none
    pallas_call x0 -> x1, Pallas kernels: none -> 0.63 us  [fast_on_device(): pl.pallas_call(finish, out_shape=(jax.ShapeDtypeStruct((nk, nb * nvec), F...]
where the time goes in v2:
time: 20.8 us; the launch traced here: 20.6 us
  Pallas kernels  19.9 us (96%)
  between operations  0.64 us (3%)
    pallas_call x1, Pallas kernels, fast_on_device(): pl.pallas_call(functools.partial(kernel, (rows, cols, nk, nv, nc, nvec, t...  19.3 us
    pallas_call x1, Pallas kernels, fast_on_device(): pl.pallas_call(finish, out_shape=(jax.ShapeDtypeStruct((nk, nb * nvec), F...  0.63 us

profile of v2, /device:TPU:0, one launch (start us, length us, event | category | flops | bytes accessed | tf_op | source)
XLA Modules:
  0.0 20.6 jit_solution(8751053477239081642)
XLA Ops:
  0.6 19.3 %shard_map.95 = (f32[2,512]{1,0:T(2,128)S(1)}, f32[32,32]{1,0:T(8,128)S(1)}) custom-call(bf16[2,16,1024]{2,1,0:T(8,128)(2,1)} %px_hbm.1, bf16[2,4,1024]{2,1,0:T(4,128)(2,1)} %cond_hbm.1, bf16[2,4,1024]{2,1,0:T(4,128)(2,1)} %val_hbm.1, f32[1,1024]{1,0:T(1,128)} %bitcast.1, f32[34,1024]{1,0:T(8,128)} %screening_hbm.1, bf16[2,512]{1,0:T(2,128)(2,1)} %vec_hbm.1, ...), custom_call_target="tpu_custom_call" | custom-call | tf_op jit(solution)/shard_map/pallas_call | solution.py:345
  19.9 0.6 %shard_map.96 = (f32[2,512]{1,0:T(2,128)}, f32[32,32]{1,0:T(8,128)}) custom-call(f32[2,512]{1,0:T(2,128)S(1)} %get-tuple-element.4.out_ref, f32[32,32]{1,0:T(8,128)S(1)} %get-tuple-element.5.alpha_ref), custom_call_target="tpu_custom_call" | custom-call | tf_op jit(solution)/shard_map/pallas_call | solution.py:381

commit v3 on v2

v3 whole, which is shorter than its diff:
```python
import functools
import math

import jax
import jax.numpy as jnp
from jax import lax
from jax.experimental import pallas as pl
from jax.experimental.pallas import tpu as pltpu
from jax.sharding import PartitionSpec as P

MX = 32
LANES = 128
MESH = pl.DeviceIdType.MESH
F32 = jnp.float32
BF16 = jnp.bfloat16


def split_pair(value):
    high = value.astype(BF16)
    return high, (value - high.astype(F32)).astype(BF16)


def dot(a, b, contract):
    return lax.dot_general(a, b, ((contract[0:1], contract[1:2]), ((), ())), preferred_element_type=F32)


def iota(shape, axis):
    return lax.broadcasted_iota(jnp.int32, shape, axis)


def one_hot(condition):
    return jnp.where(condition, 1.0, 0.0).astype(BF16)


def wide_dot(a, b, contract):
    high, low = a
    main, rest = b
    return dot(high, main, contract) + dot(low, main, contract) + dot(high, rest, contract)


def beside(*parts):
    return jnp.concatenate(parts, axis=1)


def above(*parts):
    return jnp.concatenate(parts, axis=0)


def swap_blocks(tile, lanes, rows):
    row_bit = (iota(tile.shape, 0) // rows) % 2
    lane_bit = (iota(tile.shape, 1) // lanes) % 2
    up = pltpu.roll(pltpu.roll(tile, lanes, 1), tile.shape[0] - rows, 0)
    down = pltpu.roll(pltpu.roll(tile, LANES - lanes, 1), rows, 0)
    return jnp.where(row_bit == lane_bit, tile, jnp.where(lane_bit == 1, up, down))


def fold_blocks(square, width):
    kept = jnp.where(iota(square.shape, 0) // width == iota(square.shape, 1) // width, square, 0.0)
    rows = kept[0:width]
    for at in range(width, square.shape[0], width):
        rows = rows + kept[at:at + width]
    half = rows + pltpu.roll(rows, LANES // 2, 1)
    return half + pltpu.roll(half, LANES // 4, 1)


def basis(phase, sign):
    angle = (phase % MX).astype(F32) * (2.0 * math.pi / MX)
    return (jnp.cos(angle) + jnp.sin(angle)) * (1 - 2 * (sign % 2)).astype(F32)


def kernel(
    dims, px_hbm, cond_hbm, val_hbm, coulomb_hbm, screening_hbm, vec_hbm, energy_hbm, place_hbm,
    out_ref, alpha_ref,
    px_ref, cond_ref, val_ref, coulomb_ref, screening_ref, vec_ref, energy_ref, place_ref,
    load_sem, msg_ref, slots, px_msg, px_slots, select, select_q, lam, pairs, moved, proj, out_send, out_slots, gram_slots,
    base_send, base_slot, sends, arrivals,
):
    rows, cols, nk, nv, nc, nvec, total = dims
    row, col = lax.axis_index("row"), lax.axis_index("col")
    me = row * cols + col
    count = rows * cols
    nb = nv * nc
    low_row, high_row = rows // 4, rows - rows // 4
    hosts = (high_row - low_row) * cols
    host = (row >= low_row) & (row < high_row)
    guest = jnp.logical_not(host)
    near_row = jnp.where(row < low_row, row + low_row, jnp.where(row >= high_row, row - low_row, row))
    seat = (near_row - low_row) * cols + col
    width = LANES // cols
    deep = width // 2
    unit = nk * nv
    half = LANES // 2
    sheets = count * 8
    spans = rows * LANES // hosts // width
    levels = spans * deep

    ring_rows = [row] + [lax.rem(row + step, rows) for step in range(1, rows)]
    ring_cols = [col] + [lax.rem(col + step, cols) for step in range(1, cols)]
    everyone = [(pr, pc) for i, pr in enumerate(ring_rows) for j, pc in enumerate(ring_cols) if i + j]
    host_rows = [low_row + lax.rem(near_row - low_row + step, high_row - low_row) for step in range(high_row - low_row)]
    left = lax.rem(col, 2)
    host_cols = [cols - 1 - col, lax.rem(col + 2, cols), col + 1 - 2 * left, col]
    host_peers = [(pr, pc) for pc in host_cols for pr in host_rows[::-1]]

    barrier = pltpu.get_barrier_semaphore()
    mine = pl.ds(pl.multiple_of(seat // 2 * LANES, LANES), LANES)
    loads = [
        pltpu.make_async_copy(src, dst, load_sem.at[at])
        for at, (src, dst) in enumerate((
            (val_hbm, val_ref), (cond_hbm, cond_ref), (vec_hbm, vec_ref), (place_hbm, place_ref), (px_hbm, px_ref),
            (energy_hbm, energy_ref), (screening_hbm.at[:, mine], screening_ref), (coulomb_hbm.at[:, mine], coulomb_ref)))
    ]
    for load in loads[:4]:
        load.start()

    @pl.when(host)
    def _():
        for peer in everyone:
            pl.semaphore_signal(barrier, inc=1, device_id=peer, device_id_type=MESH)

    for load in loads[4:]:
        load.start()
    row8 = iota((8, LANES), 0)
    lane8 = iota((8, LANES), 1)
    for load in loads[:4]:
        load.wait()

    vec = vec_ref[...].astype(F32)
    own = jnp.concatenate(
        [vec[k:k + 1, j * LANES:(j + 1) * LANES] for k in range(nk) for j in range(nv)], axis=0)
    tail = jnp.zeros((8, LANES), F32)
    wave = lane8 % half
    for k in range(nk):
        value = basis((wave // 2) * place_ref[k, 0], (wave % 2) * place_ref[k, 1])
        high = value.astype(BF16).astype(F32)
        tail = jnp.where(row8 == k, jnp.where(lane8 < half, high, value - high), tail)
    tail = above(tail, jnp.zeros((8, LANES), F32)).astype(BF16)
    for r in range(rows):
        span = slice(r * LANES, (r + 1) * LANES)
        turned = []
        for k in range(nk):
            tile = above(val_ref[k, :, span].astype(F32), cond_ref[k, :, span].astype(F32))
            for size in (4, 2, 1):
                tile = swap_blocks(tile, deep * size, size)
            turned.append(tile)
        flipped = [pltpu.roll(tile, 4, 0) for tile in turned]
        first_half = jnp.where(row8 < 4, turned[0], flipped[1])
        other_half = jnp.where(row8 < 4, flipped[0], turned[1])
        for q, low in enumerate((first_half, other_half)):
            msg_ref[r * 2 + q, 0:16] = above(own, low).astype(BF16)
            msg_ref[r * 2 + q, 16:32] = tail

    @pl.when(host)
    def _():
        pl.semaphore_wait(barrier, hosts - 1)

    @pl.when(guest)
    def _():
        pl.semaphore_wait(barrier, hosts)

    def main_copy(device):
        peer = (device[0] - low_row) * cols + device[1]
        return pltpu.make_async_remote_copy(
            src_ref=msg_ref.at[peer, 0:18], dst_ref=slots.at[me, 0:18],
            send_sem=sends.at[0], recv_sem=arrivals.at[0], device_id=device, device_id_type=MESH)

    def px_copy(device):
        peer = (device[0] - low_row) * cols + device[1]
        return pltpu.make_async_remote_copy(
            src_ref=px_msg.at[peer], dst_ref=px_slots.at[me],
            send_sem=sends.at[1], recv_sem=arrivals.at[1], device_id=device, device_id_type=MESH)

    def out_copy(device):
        peer = device[0] * cols + device[1]
        return pltpu.make_async_remote_copy(
            src_ref=out_send.at[peer], dst_ref=out_slots.at[seat],
            send_sem=sends.at[2], recv_sem=arrivals.at[2], device_id=device, device_id_type=MESH)

    def gram_copy(device):
        return pltpu.make_async_remote_copy(
            src_ref=gram_slots.at[seat], dst_ref=gram_slots.at[seat],
            send_sem=sends.at[3], recv_sem=arrivals.at[3], device_id=device, device_id_type=MESH)

    def base_copy():
        return pltpu.make_async_remote_copy(
            src_ref=base_send, dst_ref=base_slot,
            send_sem=sends.at[4], recv_sem=arrivals.at[4], device_id=(near_row, col), device_id_type=MESH)

    def start_all(copy, targets):
        for peer in targets:
            copy(peer).start()

    def pack(block):
        piece = block[0:8]
        for b in range(1, nc):
            piece = jnp.where(lane8 // nvec == b, block[b * 8:b * 8 + 8], piece)
        return piece

    def landed(ref, sem):
        pltpu.make_async_copy(ref, ref, sem).wait()

    def to_hosts(copy, here, there):
        start_all(copy, host_peers[:-1])

        @pl.when(guest)
        def _():
            copy(host_peers[-1]).start()

        @pl.when(host)
        def _():
            there[me] = here[seat]

    to_hosts(main_copy, msg_ref, slots)

    loads[4].wait()
    at = iota((nk * nb, nk * nb), 0)
    to = iota((nk * nb, nk * nb), 1)
    order = one_hot(to == (at % unit) // nv * nb + at % nv * nc + at // unit)
    arranged = dot(order, px_ref[...].reshape(nk * nb, px_ref.shape[2]), (1, 0))
    for r in range(rows):
        span = slice(r * LANES, (r + 1) * LANES)
        tiles = []
        for q in range(cols):
            tile = arranged[q * 8:q * 8 + 8, span]
            for b in range(cols):
                if b != q:
                    moving = pltpu.roll(arranged[b * 8:b * 8 + 8, span], (width * (b - q)) % LANES, 1)
                    tile = jnp.where(lane8 // width == b, moving, tile)
            tiles.append(tile)
        for q in range(2):
            px_msg[r * 2 + q] = above(tiles[2 * q], tiles[2 * q + 1]).astype(BF16)
    to_hosts(px_copy, px_msg, px_slots)

    loads[5].wait()
    energy = jnp.zeros((8, LANES), F32)
    for k in range(nk):
        for t in range(nb):
            energy = jnp.where((row8 == k * nv + t // nc) & (lane8 // nvec == t % nc), energy_ref[k, t], energy)
    lifted = energy * own
    high, low = split_pair(lifted)
    own_low = own.astype(BF16)
    base_send[...] = pack(fold_blocks(dot(own_low, high, (0, 0)) + dot(own_low, low, (0, 0)), nvec))

    @pl.when(guest)
    def _():
        base_copy().start()

    for load in loads[6:]:
        load.wait()

    @pl.when(host)
    def _():
        at = iota((sheets, LANES), 0)
        to = iota((sheets, LANES), 1)
        same = at // 8 == (to % half) // nk
        place = at % 8
        for j in range(nv):
            select[:, j * LANES:(j + 1) * LANES] = one_hot(same & (place == to % nk * nv + j))
        for a in range(spans):
            select[:, (nv + a) * LANES:(nv + a + 1) * LANES] = one_hot(
                same & (place == to % nk * 2 * spans + 2 * a + to // half))
        at = iota((LANES, sheets), 0)
        to = iota((LANES, sheets), 1)
        select_q[...] = one_hot((to // 8 == (at % half) // nk) & (to % 8 == at % nk))
        at = iota((LANES, LANES), 0)
        to = iota((LANES, LANES), 1)
        fold = at // 2
        angle = ((fold * ((to % half) // 2)) % MX).astype(F32) * (2.0 * math.pi / MX)
        weight = jnp.where((fold == 0) | (fold == MX // 2), 1.0, 2.0) * (1 - 2 * ((at % 2) * (to % 2))).astype(F32)
        table = jnp.where(fold <= MX // 2, jnp.cos(angle) * weight, 0.0)
        screened = above(screening_ref[...], jnp.zeros((LANES - screening_ref.shape[0], LANES), F32))
        lam[...] = wide_dot(split_pair(screened), split_pair(table), (0, 0)) * (-1.0 / (total * total))
        second_half = lax.rem(seat, 2)
        band = lam[pl.ds(pl.multiple_of(second_half * half, 8), half), :]
        lane_d = iota((deep, LANES), 1)
        spectrum = above(*[
            jnp.where(lane_d < half, band[2 * a * deep:(2 * a + 1) * deep], band[(2 * a + 1) * deep:(2 * a + 2) * deep])
            for a in range(spans)])
        raw = jnp.broadcast_to(coulomb_ref[...], (width, LANES)) * (2.0 / (total * nb))
        lane_w = iota((width, LANES), 1)
        charges = []
        for a in range(spans):
            tiles = jnp.zeros((width, LANES), F32)
            for b in range(cols):
                for q in range(2):
                    shift = (width * (b - 2 * q - a)) % LANES
                    moving = raw if shift == 0 else pltpu.roll(raw, shift, 1)
                    tiles = jnp.where((lane_w // width == b) & (second_half == q), moving, tiles)
            charges.append(tiles)

        landed(slots.at[0:count - 1, 0:18], arrivals.at[0])
        got = slots[...].astype(F32)
        own_all, rest_all, wave_all = [
            got[:, 8 * part:8 * part + 8].reshape(sheets, LANES) for part in range(3)]
        own_all, rest_all = own_all.astype(BF16), rest_all.astype(BF16)
        wave_all = jnp.where(iota((sheets, LANES), 0) % 8 < nk, wave_all, 0.0).astype(BF16)
        factors = dot(rest_all, select[:, nv * LANES:], (0, 0))
        spread = dot(own_all, select[:, 0:nv * LANES], (0, 0))
        for v in range(nv):
            for c in range(nc):
                for a in range(spans):
                    lanes = slice(a * LANES, (a + 1) * LANES)
                    joined = (
                        factors[v * deep:(v + 1) * deep, lanes] * factors[half + c * deep:half + (c + 1) * deep, lanes])
                    pairs[v * nc + c, a * deep:(a + 1) * deep] = joined.astype(BF16).astype(F32)
        for t in range(nb):
            moved[t] = spread[t % nc * nvec:(t % nc + 1) * nvec, t // nc * LANES:(t // nc + 1) * LANES]
        waves = dot(select_q[...], wave_all, (1, 0))
        crossed = pltpu.roll(waves, half, 1)
        first = (at < half) & (to < half)
        second = (at >= half) & (to >= half)
        main = jnp.where(first, waves, jnp.where(second, crossed, 0.0)).astype(BF16)
        fine = jnp.where(first, crossed, jnp.where(second, waves, 0.0)).astype(BF16)
        none = jnp.zeros((LANES, LANES), BF16)
        ahead = above(beside(main, fine), beside(main, none))
        astern = above(beside(main, main), beside(fine, none))

        def through(values, weights, contract):
            both = dot(beside(*split_pair(values)), weights, contract)
            return both[:, 0:LANES] + both[:, LANES:]

        group = 2
        for first_l in range(0, levels, group):
            sums_l = [None] * group
            for t in range(nb):
                for u in range(group):
                    term = pairs[t, first_l + u:first_l + u + 1, :] * moved[t]
                    sums_l[u] = term if t == 0 else sums_l[u] + term
            for u in range(group):
                proj[first_l + u] = sums_l[u]
        spectral = through(proj[...].reshape(levels * nvec, LANES), ahead, (1, 0)).reshape(levels, nvec, LANES)
        scaled = spectral * spectrum[:, None, :]
        sides = [
            split_pair(jnp.concatenate([side[l] for l in range(levels)], axis=1)) for side in (spectral, scaled)]
        gram = wide_dot(*sides, (1, 1))

        landed(px_slots.at[0:count - 1], arrivals.at[1])
        taken_px = px_slots[...].astype(F32)
        exchange = beside(*[
            taken_px[:, 8 * a:8 * a + 8].reshape(sheets, LANES).astype(BF16) for a in range(spans)])
        crowd = dot(own_all, exchange, (0, 0))
        densities = [fold_blocks(crowd[:, a * LANES:(a + 1) * LANES], nvec) for a in range(spans)]
        charged = [density * charge for density, charge in zip(densities, charges)]
        gram = gram + wide_dot(
            split_pair(beside(*densities)), split_pair(beside(*charged) * (1.0 / cols)), (1, 1))
        landed(base_slot, arrivals.at[4])
        gram_slots[seat] = (
            base_send[...] + base_slot[...] + pack(jnp.concatenate([gram] * nc, axis=1))).astype(BF16)
        start_all(gram_copy, everyone)

        proj[...] = through(scaled.reshape(levels * nvec, LANES), astern, (1, 1)).reshape(levels, nvec, LANES)
        blocks = beside(*[
            jnp.where(at // nvec == to // width, jnp.concatenate([charge] * (LANES // nvec), axis=0), 0.0)
            for charge in charged])
        whole = dot(exchange, above(*split_pair(blocks)), (1, 1))
        for first_t in range(0, nb, group):
            sums_t = [None] * group
            for l in range(levels):
                for u in range(group):
                    term = pairs[first_t + u, l:l + 1, :] * proj[l]
                    sums_t[u] = term if l == 0 else sums_t[u] + term
            for u in range(group):
                moved[first_t + u] = sums_t[u]
        placed = jnp.concatenate(
            [jnp.concatenate([moved[j * nc + c] for c in range(nc)], axis=0) for j in range(nv)], axis=1)
        whole = whole + dot(select[:, 0:nv * LANES], above(*split_pair(placed)), (1, 1))
        whole = whole[:, 0:LANES] + whole[:, LANES:]
        out_send[...] = whole.astype(BF16).reshape(count, 8, LANES)
        start_all(out_copy, everyone)
        out_slots[seat] = out_send[me]

    def each(run):
        @pl.when(host)
        def _():
            run(hosts - 1)

        @pl.when(guest)
        def _():
            run(hosts)

    each(lambda n: landed(gram_slots.at[0:n], arrivals.at[3]))
    sums = jnp.sum(gram_slots[...].astype(F32), axis=0) * (1.0 / (total * nb))
    turns = [sums] + [pltpu.roll(sums, b * nvec, 1) for b in range(1, nc)]
    for b in range(nc):
        alpha_ref[b * 8:b * 8 + 8] = turns[(-b) % nc][:, 0:nvec]
    mixed = jnp.concatenate(
        [jnp.where(lane8 // nvec == q, turns[(q - b) % nc], 0.0) for q in range(nc) for b in range(nc)], axis=0)
    high, low = split_pair(mixed)
    rest = lifted - dot(own_low, high, (1, 0)) - dot(own_low, low, (1, 0))

    each(lambda n: landed(out_slots.at[0:n], arrivals.at[2]))
    residual = rest + jnp.sum(out_slots[...].astype(F32), axis=0)
    for j in range(nv):
        out_ref[:, j * LANES:(j + 1) * LANES] = jnp.concatenate(
            [residual[k * nv + j:k * nv + j + 1] for k in range(nk)], axis=0)

    def drain(n):
        landed(slots.at[0:n, 0:18], sends.at[0])
        landed(px_slots.at[0:n], sends.at[1])

    each(drain)

    @pl.when(guest)
    def _():
        landed(base_slot, sends.at[4])

    @pl.when(host)
    def _():
        landed(out_send.at[0:count - 1], sends.at[2])
        landed(out_send.at[0:count - 1], sends.at[3])


def finish(out_ref, alpha_ref, out_hbm, alpha_hbm, sems):
    copies = [
        pltpu.make_async_copy(src, dst, sems.at[at])
        for at, (src, dst) in enumerate(((out_ref, out_hbm), (alpha_ref, alpha_hbm)))]
    for copy in copies:
        copy.start()
    for copy in copies:
        copy.wait()


def fast_on_device(pair_exchange, conduction, valence, coulomb, screening, energies, vectors, k_coords):
    nk, nb, planes = pair_exchange.shape
    nv, nc = valence.shape[1], conduction.shape[1]
    nvec = vectors.shape[1] // nb
    rows, cols = lax.axis_size("row"), lax.axis_size("col")
    count = rows * cols
    total = nk * count
    hosts = count // 2
    width = LANES // cols
    spans = planes // hosts // width
    levels = spans * width // 2
    vmem = pl.BlockSpec(memory_space=pltpu.VMEM)
    dma = pltpu.SemaphoreType.DMA
    results = pl.pallas_call(
        functools.partial(kernel, (rows, cols, nk, nv, nc, nvec, total)),
        out_shape=(
            pltpu.VMEM((nk, nb * nvec), F32),
            pltpu.VMEM((nvec, nvec), F32),
        ),
        in_specs=[pl.BlockSpec(memory_space=pl.ANY)] * 8,
        out_specs=(vmem, vmem),
        scratch_shapes=[
            pltpu.VMEM(pair_exchange.shape, BF16),
            pltpu.VMEM(conduction.shape, BF16),
            pltpu.VMEM(valence.shape, BF16),
            pltpu.VMEM((1, LANES), F32),
            pltpu.VMEM((screening.shape[0], LANES), F32),
            pltpu.VMEM(vectors.shape, BF16),
            pltpu.SMEM(energies.shape, F32),
            pltpu.SMEM(k_coords.shape, jnp.int32),
            dma((8,)),
            pltpu.VMEM((hosts, 32, LANES), BF16),
            pltpu.VMEM((count, 32, LANES), BF16),
            pltpu.VMEM((hosts, 16, LANES), BF16),
            pltpu.VMEM((count, 16, LANES), BF16),
            pltpu.VMEM((count * 8, (nv + spans) * LANES), BF16),
            pltpu.VMEM((LANES, count * 8), BF16),
            pltpu.VMEM((LANES, LANES), F32),
            pltpu.VMEM((nb, levels, LANES), F32),
            pltpu.VMEM((nb, nvec, LANES), F32),
            pltpu.VMEM((levels, nvec, LANES), F32),
            pltpu.VMEM((count, 8, LANES), BF16),
            pltpu.VMEM((hosts, 8, LANES), BF16),
            pltpu.VMEM((hosts, 8, LANES), BF16),
            pltpu.VMEM((8, LANES), F32),
            pltpu.VMEM((8, LANES), F32),
            dma((5,)), dma((5,)),
        ],
        compiler_params=pltpu.CompilerParams(collective_id=0, has_side_effects=True),
    )(pair_exchange, conduction, valence, coulomb.reshape(1, planes), screening, vectors, energies, k_coords)
    return pl.pallas_call(
        finish,
        out_shape=(jax.ShapeDtypeStruct((nk, nb * nvec), F32), jax.ShapeDtypeStruct((nvec, nvec), F32)),
        in_specs=[vmem, vmem],
        out_specs=(pl.BlockSpec(memory_space=pl.ANY), pl.BlockSpec(memory_space=pl.ANY)),
        scratch_shapes=[dma((2,))],
    )(*[pltpu.with_memory_space_constraint(result, pltpu.VMEM) for result in results])


highest = lax.Precision.HIGHEST


def pair_factors(conduction, valence):
    count, valence_count, plane_count = valence.shape
    joined = (
        valence.astype(jnp.float32)[:, :, None, :] * conduction.astype(jnp.float32)[:, None, :, :]
    )
    return joined.reshape(count, valence_count * conduction.shape[1], plane_count).astype(
        jnp.bfloat16
    )


def transfer_index(rows_at, cols_at, mesh_cols):
    delta_first = jnp.mod(rows_at[:, None, 0] - cols_at[None, :, 0], MX)
    delta_second = jnp.mod(rows_at[:, None, 1] - cols_at[None, :, 1], mesh_cols)
    fold_first = jnp.minimum(delta_first, MX - delta_first)
    fold_second = jnp.minimum(delta_second, mesh_cols - delta_second)
    return (fold_first * (mesh_cols // 2 + 1) + fold_second).astype(jnp.int32)


def on_device(pair_exchange, conduction, valence, coulomb, screening, energies, vectors, k_coords):
    local_count, band_count, plane_count = pair_exchange.shape
    vector_count = vectors.shape[1] // band_count
    row_count = lax.axis_size("row")
    col_count = lax.axis_size("col")
    total_count = local_count * row_count * col_count
    mesh_cols = total_count // MX
    moving = vectors.reshape(local_count, band_count, vector_count)
    partial_density = jnp.einsum(
        "ktg,ktn->gn", pair_exchange, moving, preferred_element_type=jnp.float32
    )
    density = lax.psum(partial_density, ("row", "col"))
    block_size = 128
    sweeps = plane_count // block_size
    col_cond, col_val, col_vec, col_at = (
        lax.all_gather(conduction, "row", axis=0, tiled=True),
        lax.all_gather(valence, "row", axis=0, tiled=True),
        lax.all_gather(vectors, "row", axis=0, tiled=True),
        lax.all_gather(k_coords, "row", axis=0, tiled=True),
    )
    row_cond, row_val, row_at = (
        lax.all_gather(conduction, "col", axis=0, tiled=True),
        lax.all_gather(valence, "col", axis=0, tiled=True),
        lax.all_gather(k_coords, "col", axis=0, tiled=True),
    )
    row_pairs = pair_factors(row_cond, row_val)
    col_pairs = pair_factors(col_cond, col_val)
    indices = transfer_index(row_at, col_at, mesh_cols)
    col_moving = col_vec.reshape(-1, band_count, vector_count)

    def square_sweep(sweep_index, running):
        anchor = sweep_index * block_size
        coupling = jnp.take(
            lax.dynamic_slice_in_dim(screening, anchor, block_size, 1), indices, axis=0
        )
        row_block = lax.dynamic_slice_in_dim(row_pairs, anchor, block_size, 2)
        col_block = lax.dynamic_slice_in_dim(col_pairs, anchor, block_size, 2)
        col_proj = jnp.einsum(
            "ktg,ktn->kng", col_block, col_moving, preferred_element_type=jnp.float32
        )
        potential = jnp.einsum("ijg,jng->ing", coupling, col_proj, precision=highest)
        return running + jnp.einsum(
            "ktg,kng->ktn", row_block.astype(jnp.float32), potential, precision=highest
        )

    forward = lax.fori_loop(
        0,
        sweeps,
        square_sweep,
        jnp.zeros((row_pairs.shape[0], band_count, vector_count), jnp.float32),
    )
    owned = lax.psum_scatter(
        forward.reshape(col_count, local_count, band_count, vector_count),
        "col",
        scatter_dimension=0,
        tiled=True,
    )[0]
    moving_wide = moving.astype(jnp.float32)
    exchange_term = jnp.einsum(
        "ktg,gn->ktn", pair_exchange.astype(jnp.float32) * coulomb, density, precision=highest
    )
    applied = (
        energies[:, :, None] * moving_wide
        + 2.0 / (total_count * band_count) * exchange_term
        - owned / total_count
    )
    gram = jnp.einsum("ktm,ktn->mn", moving_wide, applied, precision=highest)
    alpha = lax.psum(gram, ("row", "col")) / (total_count * band_count)
    residual = applied - jnp.einsum("ktm,mn->ktn", moving_wide, alpha, precision=highest)
    return (residual.reshape(local_count, band_count * vector_count), alpha)


def fits(args, mesh):
    pair_exchange, conduction, valence, _, screening, _, vectors, _ = args
    rows, cols = mesh.shape["row"], mesh.shape["col"]
    points, nb, planes = pair_exchange.shape
    nk = points // (rows * cols)
    nv, nc = valence.shape[1], conduction.shape[1]
    nvec = vectors.shape[1] // nb
    return (
        planes == rows * LANES and rows == 8 and cols == 4 and rows * cols * nk * 2 == LANES and nk == 2 and nv == 4 and nc == 4
        and nc * nvec == LANES and points == 2 * MX and screening.shape[0] == MX + 2
    )


def solution(mesh):
    in_specs = (
        P(("row", "col"), None, None),
        P(("row", "col"), None, None),
        P(("row", "col"), None, None),
        P(),
        P(),
        P(("row", "col"), None),
        P(("row", "col"), None),
        P(("row", "col"), None),
    )
    out_specs = (P(("row", "col"), None), P())

    def run(*args):
        body = fast_on_device if fits(args, mesh) else on_device
        return jax.shard_map(
            body, mesh=mesh, in_specs=in_specs, out_specs=out_specs, check_vma=False
        )(*args)

    return run
```

time: 20.8 us -> 19.2 us (0.923)
  Pallas kernels: 19.9 us -> 18.3 us
    pallas_call x1, Pallas kernels: 19.3 us -> 17.7 us  [fast_on_device(): pl.pallas_call(functools.partial(kernel, (rows, cols, nk, nv, nc, nvec, t...]
where the time goes in v3:
time: 19.2 us; the launch traced here: 19 us
  Pallas kernels  18.3 us (95%)
  between operations  0.64 us (3%)
    pallas_call x1, Pallas kernels, fast_on_device(): pl.pallas_call(functools.partial(kernel, (rows, cols, nk, nv, nc, nvec, t...  17.7 us
    pallas_call x1, Pallas kernels, fast_on_device(): pl.pallas_call(finish, out_shape=(jax.ShapeDtypeStruct((nk, nb * nvec), F...  0.63 us

profile of v3, /device:TPU:0, one launch (start us, length us, event | category | flops | bytes accessed | tf_op | source)
XLA Modules:
  0.0 19.0 jit_solution(1925343579308732455)
XLA Ops:
  0.6 17.7 %shard_map.95 = (f32[2,512]{1,0:T(2,128)S(1)}, f32[32,32]{1,0:T(8,128)S(1)}) custom-call(bf16[2,16,1024]{2,1,0:T(8,128)(2,1)} %px_hbm.1, bf16[2,4,1024]{2,1,0:T(4,128)(2,1)} %cond_hbm.1, bf16[2,4,1024]{2,1,0:T(4,128)(2,1)} %val_hbm.1, f32[1,1024]{1,0:T(1,128)} %bitcast.1, f32[34,1024]{1,0:T(8,128)} %screening_hbm.1, bf16[2,512]{1,0:T(2,128)(2,1)} %vec_hbm.1, ...), custom_call_target="tpu_custom_call" | custom-call | tf_op jit(solution)/shard_map/pallas_call | solution.py:436
  18.3 0.6 %shard_map.96 = (f32[2,512]{1,0:T(2,128)}, f32[32,32]{1,0:T(8,128)}) custom-call(f32[2,512]{1,0:T(2,128)S(1)} %get-tuple-element.4.out_ref, f32[32,32]{1,0:T(8,128)S(1)} %get-tuple-element.5.alpha_ref), custom_call_target="tpu_custom_call" | custom-call | tf_op jit(solution)/shard_map/pallas_call | solution.py:473

commit v4 on v3

--- a/solution.py
+++ b/solution.py
@@ -97,6 +97,16 @@
     ring_rows = [row] + [lax.rem(row + step, rows) for step in range(1, rows)]
     ring_cols = [col] + [lax.rem(col + step, cols) for step in range(1, cols)]
     everyone = [(pr, pc) for i, pr in enumerate(ring_rows) for j, pc in enumerate(ring_cols) if i + j]
+    late = jnp.logical_and(col == 0, row < 2)
+    rank = jnp.where(late, 0, me - 1 - (me > cols).astype(jnp.int32))
+
+    def turned_to(step):
+        at = rank + step
+        at = jnp.where(at >= count - 2, at - (count - 2), at)
+        spot = at + 1 + (at >= cols - 1).astype(jnp.int32)
+        return spot // cols, lax.rem(spot, cols)
+
+    leading = [(0, 0), (1, 0)] + [turned_to(step) for step in range(1, count - 2)]
     host_rows = [low_row + lax.rem(near_row - low_row + step, high_row - low_row) for step in range(high_row - low_row)]
     left = lax.rem(col, 2)
     host_cols = [cols - 1 - col, lax.rem(col + 2, cols), col + 1 - 2 * left, col]
@@ -115,7 +125,7 @@
 
     @pl.when(host)
     def _():
-        for peer in everyone:
+        for peer in leading:
             pl.semaphore_signal(barrier, inc=1, device_id=peer, device_id_type=MESH)
 
     for load in loads[4:]:
@@ -150,68 +160,6 @@
             msg_ref[r * 2 + q, 0:16] = above(own, low).astype(BF16)
             msg_ref[r * 2 + q, 16:32] = tail
 
-    @pl.when(host)
-    def _():
-        pl.semaphore_wait(barrier, hosts - 1)
-
-    @pl.when(guest)
-    def _():
-        pl.semaphore_wait(barrier, hosts)
-
-    def main_copy(device):
-        peer = (device[0] - low_row) * cols + device[1]
-        return pltpu.make_async_remote_copy(
-            src_ref=msg_ref.at[peer, 0:18], dst_ref=slots.at[me, 0:18],
-            send_sem=sends.at[0], recv_sem=arrivals.at[0], device_id=device, device_id_type=MESH)
-
-    def px_copy(device):
-        peer = (device[0] - low_row) * cols + device[1]
-        return pltpu.make_async_remote_copy(
-            src_ref=px_msg.at[peer], dst_ref=px_slots.at[me],
-            send_sem=sends.at[1], recv_sem=arrivals.at[1], device_id=device, device_id_type=MESH)
-
-    def out_copy(device):
-        peer = device[0] * cols + device[1]
-        return pltpu.make_async_remote_copy(
-            src_ref=out_send.at[peer], dst_ref=out_slots.at[seat],
-            send_sem=sends.at[2], recv_sem=arrivals.at[2], device_id=device, device_id_type=MESH)
-
-    def gram_copy(device):
-        return pltpu.make_async_remote_copy(
-            src_ref=gram_slots.at[seat], dst_ref=gram_slots.at[seat],
-            send_sem=sends.at[3], recv_sem=arrivals.at[3], device_id=device, device_id_type=MESH)
-
-    def base_copy():
-        return pltpu.make_async_remote_copy(
-            src_ref=base_send, dst_ref=base_slot,
-            send_sem=sends.at[4], recv_sem=arrivals.at[4], device_id=(near_row, col), device_id_type=MESH)
-
-    def start_all(copy, targets):
-        for peer in targets:
-            copy(peer).start()
-
-    def pack(block):
-        piece = block[0:8]
-        for b in range(1, nc):
-            piece = jnp.where(lane8 // nvec == b, block[b * 8:b * 8 + 8], piece)
-        return piece
-
-    def landed(ref, sem):
-        pltpu.make_async_copy(ref, ref, sem).wait()
-
-    def to_hosts(copy, here, there):
-        start_all(copy, host_peers[:-1])
-
-        @pl.when(guest)
-        def _():
-            copy(host_peers[-1]).start()
-
-        @pl.when(host)
-        def _():
-            there[me] = here[seat]
-
-    to_hosts(main_copy, msg_ref, slots)
-
     loads[4].wait()
     at = iota((nk * nb, nk * nb), 0)
     to = iota((nk * nb, nk * nb), 1)
@@ -229,6 +177,68 @@
             tiles.append(tile)
         for q in range(2):
             px_msg[r * 2 + q] = above(tiles[2 * q], tiles[2 * q + 1]).astype(BF16)
+    @pl.when(host)
+    def _():
+        pl.semaphore_wait(barrier, hosts - 1)
+
+    @pl.when(guest)
+    def _():
+        pl.semaphore_wait(barrier, hosts)
+
+    def main_copy(device):
+        peer = (device[0] - low_row) * cols + device[1]
+        return pltpu.make_async_remote_copy(
+            src_ref=msg_ref.at[peer, 0:18], dst_ref=slots.at[me, 0:18],
+            send_sem=sends.at[0], recv_sem=arrivals.at[0], device_id=device, device_id_type=MESH)
+
+    def px_copy(device):
+        peer = (device[0] - low_row) * cols + device[1]
+        return pltpu.make_async_remote_copy(
+            src_ref=px_msg.at[peer], dst_ref=px_slots.at[me],
+            send_sem=sends.at[1], recv_sem=arrivals.at[1], device_id=device, device_id_type=MESH)
+
+    def out_copy(device):
+        peer = device[0] * cols + device[1]
+        return pltpu.make_async_remote_copy(
+            src_ref=out_send.at[peer], dst_ref=out_slots.at[seat],
+            send_sem=sends.at[2], recv_sem=arrivals.at[2], device_id=device, device_id_type=MESH)
+
+    def gram_copy(device):
+        return pltpu.make_async_remote_copy(
+            src_ref=gram_slots.at[seat], dst_ref=gram_slots.at[seat],
+            send_sem=sends.at[3], recv_sem=arrivals.at[3], device_id=device, device_id_type=MESH)
+
+    def base_copy():
+        return pltpu.make_async_remote_copy(
+            src_ref=base_send, dst_ref=base_slot,
+            send_sem=sends.at[4], recv_sem=arrivals.at[4], device_id=(near_row, col), device_id_type=MESH)
+
+    def start_all(copy, targets):
+        for peer in targets:
+            copy(peer).start()
+
+    def pack(block):
+        piece = block[0:8]
+        for b in range(1, nc):
+            piece = jnp.where(lane8 // nvec == b, block[b * 8:b * 8 + 8], piece)
+        return piece
+
+    def landed(ref, sem):
+        pltpu.make_async_copy(ref, ref, sem).wait()
+
+    def to_hosts(copy, here, there):
+        start_all(copy, host_peers[:-1])
+
+        @pl.when(guest)
+        def _():
+            copy(host_peers[-1]).start()
+
+        @pl.when(host)
+        def _():
+            there[me] = here[seat]
+
+    to_hosts(main_copy, msg_ref, slots)
+
     to_hosts(px_copy, px_msg, px_slots)
 
     loads[5].wait()
@@ -343,17 +353,25 @@
         charged = [density * charge for density, charge in zip(densities, charges)]
         gram = gram + wide_dot(
             split_pair(beside(*densities)), split_pair(beside(*charged) * (1.0 / cols)), (1, 1))
+        proj[...] = through(scaled.reshape(levels * nvec, LANES), astern, (1, 1)).reshape(levels, nvec, LANES)
+        for first_t in range(0, nb // 2, group):
+            sums_t = [None] * group
+            for l in range(levels):
+                for u in range(group):
+                    term = pairs[first_t + u, l:l + 1, :] * proj[l]
+                    sums_t[u] = term if l == 0 else sums_t[u] + term
+            for u in range(group):
+                moved[first_t + u] = sums_t[u]
         landed(base_slot, arrivals.at[4])
         gram_slots[seat] = (
             base_send[...] + base_slot[...] + pack(jnp.concatenate([gram] * nc, axis=1))).astype(BF16)
-        start_all(gram_copy, everyone)
-
-        proj[...] = through(scaled.reshape(levels * nvec, LANES), astern, (1, 1)).reshape(levels, nvec, LANES)
+        start_all(gram_copy, leading[:2])
+
         blocks = beside(*[
             jnp.where(at // nvec == to // width, jnp.concatenate([charge] * (LANES // nvec), axis=0), 0.0)
             for charge in charged])
         whole = dot(exchange, above(*split_pair(blocks)), (1, 1))
-        for first_t in range(0, nb, group):
+        for first_t in range(nb // 2, nb, group):
             sums_t = [None] * group
             for l in range(levels):
                 for u in range(group):
@@ -365,8 +383,9 @@
             [jnp.concatenate([moved[j * nc + c] for c in range(nc)], axis=0) for j in range(nv)], axis=1)
         whole = whole + dot(select[:, 0:nv * LANES], above(*split_pair(placed)), (1, 1))
         whole = whole[:, 0:LANES] + whole[:, LANES:]
-        out_send[...] = whole.astype(BF16).reshape(count, 8, LANES)
-        start_all(out_copy, everyone)
+        out_send[...] = whole.reshape(count, 8, LANES)
+        start_all(out_copy, leading)
+        start_all(gram_copy, leading[2:])
         out_slots[seat] = out_send[me]
 
     def each(run):
@@ -389,7 +408,7 @@
     rest = lifted - dot(own_low, high, (1, 0)) - dot(own_low, low, (1, 0))
 
     each(lambda n: landed(out_slots.at[0:n], arrivals.at[2]))
-    residual = rest + jnp.sum(out_slots[...].astype(F32), axis=0)
+    residual = rest + jnp.sum(out_slots[...], axis=0)
     for j in range(nv):
         out_ref[:, j * LANES:(j + 1) * LANES] = jnp.concatenate(
             [residual[k * nv + j:k * nv + j + 1] for k in range(nk)], axis=0)
@@ -407,7 +426,7 @@
     @pl.when(host)
     def _():
         landed(out_send.at[0:count - 1], sends.at[2])
-        landed(out_send.at[0:count - 1], sends.at[3])
+        landed(slots.at[0:count - 1, 0:8], sends.at[3])
 
 
 def finish(out_ref, alpha_ref, out_hbm, alpha_hbm, sems):
@@ -461,8 +480,8 @@
             pltpu.VMEM((nb, levels, LANES), F32),
             pltpu.VMEM((nb, nvec, LANES), F32),
             pltpu.VMEM((levels, nvec, LANES), F32),
-            pltpu.VMEM((count, 8, LANES), BF16),
-            pltpu.VMEM((hosts, 8, LANES), BF16),
+            pltpu.VMEM((count, 8, LANES), F32),
+            pltpu.VMEM((hosts, 8, LANES), F32),
             pltpu.VMEM((hosts, 8, LANES), BF16),
             pltpu.VMEM((8, LANES), F32),
             pltpu.VMEM((8, LANES), F32),

time: 19.2 us -> 18.9 us (0.984)
  Pallas kernels: 18.3 us -> 18 us
    pallas_call x1, Pallas kernels: 17.7 us -> 17.3 us  [fast_on_device(): pl.pallas_call(functools.partial(kernel, (rows, cols, nk, nv, nc, nvec, t...]
where the time goes in v4:
time: 18.9 us; the launch traced here: 18.6 us
  Pallas kernels  18 us (95%)
  between operations  0.64 us (3%)
    pallas_call x1, Pallas kernels, fast_on_device(): pl.pallas_call(functools.partial(kernel, (rows, cols, nk, nv, nc, nvec, t...  17.3 us
    pallas_call x1, Pallas kernels, fast_on_device(): pl.pallas_call(finish, out_shape=(jax.ShapeDtypeStruct((nk, nb * nvec), F...  0.63 us

profile of v4, /device:TPU:0, one launch (start us, length us, event | category | flops | bytes accessed | tf_op | source)
XLA Modules:
  0.0 18.6 jit_solution(16790355697176854056)
XLA Ops:
  0.6 17.3 %shard_map.95 = (f32[2,512]{1,0:T(2,128)S(1)}, f32[32,32]{1,0:T(8,128)S(1)}) custom-call(bf16[2,16,1024]{2,1,0:T(8,128)(2,1)} %px_hbm.1, bf16[2,4,1024]{2,1,0:T(4,128)(2,1)} %cond_hbm.1, bf16[2,4,1024]{2,1,0:T(4,128)(2,1)} %val_hbm.1, f32[1,1024]{1,0:T(1,128)} %bitcast.1, f32[34,1024]{1,0:T(8,128)} %screening_hbm.1, bf16[2,512]{1,0:T(2,128)(2,1)} %vec_hbm.1, ...), custom_call_target="tpu_custom_call" | custom-call | tf_op jit(solution)/shard_map/pallas_call | solution.py:455
  18.0 0.6 %shard_map.96 = (f32[2,512]{1,0:T(2,128)}, f32[32,32]{1,0:T(8,128)}) custom-call(f32[2,512]{1,0:T(2,128)S(1)} %get-tuple-element.4.out_ref, f32[32,32]{1,0:T(8,128)S(1)} %get-tuple-element.5.alpha_ref), custom_call_target="tpu_custom_call" | custom-call | tf_op jit(solution)/shard_map/pallas_call | solution.py:492

commit v5 on v4

--- a/solution.py
+++ b/solution.py
@@ -97,16 +97,8 @@
     ring_rows = [row] + [lax.rem(row + step, rows) for step in range(1, rows)]
     ring_cols = [col] + [lax.rem(col + step, cols) for step in range(1, cols)]
     everyone = [(pr, pc) for i, pr in enumerate(ring_rows) for j, pc in enumerate(ring_cols) if i + j]
-    late = jnp.logical_and(col == 0, row < 2)
-    rank = jnp.where(late, 0, me - 1 - (me > cols).astype(jnp.int32))
-
-    def turned_to(step):
-        at = rank + step
-        at = jnp.where(at >= count - 2, at - (count - 2), at)
-        spot = at + 1 + (at >= cols - 1).astype(jnp.int32)
-        return spot // cols, lax.rem(spot, cols)
-
-    leading = [(0, 0), (1, 0)] + [turned_to(step) for step in range(1, count - 2)]
+    signalled = [
+        (jnp.where(me == at, rows - 1, at // cols), jnp.where(me == at, cols - 1, at % cols)) for at in range(count - 1)]
     host_rows = [low_row + lax.rem(near_row - low_row + step, high_row - low_row) for step in range(high_row - low_row)]
     left = lax.rem(col, 2)
     host_cols = [cols - 1 - col, lax.rem(col + 2, cols), col + 1 - 2 * left, col]
@@ -125,7 +117,7 @@
 
     @pl.when(host)
     def _():
-        for peer in leading:
+        for peer in signalled:
             pl.semaphore_signal(barrier, inc=1, device_id=peer, device_id_type=MESH)
 
     for load in loads[4:]:
@@ -260,6 +252,16 @@
 
     @pl.when(host)
     def _():
+        late = jnp.logical_and(col == 0, row < 2)
+        rank = jnp.where(late, 0, me - 1 - (me > cols).astype(jnp.int32))
+
+        def turned_to(step):
+            at = rank + step
+            at = jnp.where(at >= count - 2, at - (count - 2), at)
+            spot = at + 1 + (at >= cols - 1).astype(jnp.int32)
+            return spot // cols, lax.rem(spot, cols)
+
+        leading = [(0, 0), (1, 0)] + [turned_to(step) for step in range(1, count - 2)]
         at = iota((sheets, LANES), 0)
         to = iota((sheets, LANES), 1)
         same = at // 8 == (to % half) // nk
@@ -364,7 +366,7 @@
                 moved[first_t + u] = sums_t[u]
         landed(base_slot, arrivals.at[4])
         gram_slots[seat] = (
-            base_send[...] + base_slot[...] + pack(jnp.concatenate([gram] * nc, axis=1))).astype(BF16)
+            base_send[...] + base_slot[...] + pack(jnp.concatenate([gram] * nc, axis=1)))
         start_all(gram_copy, leading[:2])
 
         blocks = beside(*[
@@ -398,7 +400,7 @@
             run(hosts)
 
     each(lambda n: landed(gram_slots.at[0:n], arrivals.at[3]))
-    sums = jnp.sum(gram_slots[...].astype(F32), axis=0) * (1.0 / (total * nb))
+    sums = jnp.sum(gram_slots[...], axis=0) * (1.0 / (total * nb))
     turns = [sums] + [pltpu.roll(sums, b * nvec, 1) for b in range(1, nc)]
     for b in range(nc):
         alpha_ref[b * 8:b * 8 + 8] = turns[(-b) % nc][:, 0:nvec]
@@ -426,7 +428,7 @@
     @pl.when(host)
     def _():
         landed(out_send.at[0:count - 1], sends.at[2])
-        landed(slots.at[0:count - 1, 0:8], sends.at[3])
+        landed(out_send.at[0:count - 1], sends.at[3])
 
 
 def finish(out_ref, alpha_ref, out_hbm, alpha_hbm, sems):
@@ -482,7 +484,7 @@
             pltpu.VMEM((levels, nvec, LANES), F32),
             pltpu.VMEM((count, 8, LANES), F32),
             pltpu.VMEM((hosts, 8, LANES), F32),
-            pltpu.VMEM((hosts, 8, LANES), BF16),
+            pltpu.VMEM((hosts, 8, LANES), F32),
             pltpu.VMEM((8, LANES), F32),
             pltpu.VMEM((8, LANES), F32),
             dma((5,)), dma((5,)),

time: 18.9 us -> 18.7 us (0.989)
  Pallas kernels: 18 us -> 17.8 us
where the time goes in v5:
time: 18.7 us; the launch traced here: 18.5 us
  Pallas kernels  17.8 us (95%)
  between operations  0.64 us (3%)
    pallas_call x1, Pallas kernels, fast_on_device(): pl.pallas_call(functools.partial(kernel, (rows, cols, nk, nv, nc, nvec, t...  17.2 us
    pallas_call x1, Pallas kernels, fast_on_device(): pl.pallas_call(finish, out_shape=(jax.ShapeDtypeStruct((nk, nb * nvec), F...  0.63 us

profile of v5, /device:TPU:0, one launch (start us, length us, event | category | flops | bytes accessed | tf_op | source)
XLA Modules:
  0.0 18.5 jit_solution(14834452136139657091)
XLA Ops:
  0.6 17.2 %shard_map.95 = (f32[2,512]{1,0:T(2,128)S(1)}, f32[32,32]{1,0:T(8,128)S(1)}) custom-call(bf16[2,16,1024]{2,1,0:T(8,128)(2,1)} %px_hbm.1, bf16[2,4,1024]{2,1,0:T(4,128)(2,1)} %cond_hbm.1, bf16[2,4,1024]{2,1,0:T(4,128)(2,1)} %val_hbm.1, f32[1,1024]{1,0:T(1,128)} %bitcast.1, f32[34,1024]{1,0:T(8,128)} %screening_hbm.1, bf16[2,512]{1,0:T(2,128)(2,1)} %vec_hbm.1, ...), custom_call_target="tpu_custom_call" | custom-call | tf_op jit(solution)/shard_map/pallas_call | solution.py:457
  17.8 0.6 %shard_map.96 = (f32[2,512]{1,0:T(2,128)}, f32[32,32]{1,0:T(8,128)}) custom-call(f32[2,512]{1,0:T(2,128)S(1)} %get-tuple-element.4.out_ref, f32[32,32]{1,0:T(8,128)S(1)} %get-tuple-element.5.alpha_ref), custom_call_target="tpu_custom_call" | custom-call | tf_op jit(solution)/shard_map/pallas_call | solution.py:494

commit v6 on v5

--- a/solution.py
+++ b/solution.py
@@ -331,6 +331,10 @@
             both = dot(beside(*split_pair(values)), weights, contract)
             return both[:, 0:LANES] + both[:, LANES:]
 
+        def unfold(first_j, last_j):
+            placed = beside(*[above(*[moved[j * nc + c] for c in range(nc)]) for j in range(first_j, last_j)])
+            return dot(select[:, first_j * LANES:last_j * LANES], above(*split_pair(placed)), (1, 1))
+
         group = 2
         for first_l in range(0, levels, group):
             sums_l = [None] * group
@@ -373,7 +377,8 @@
             jnp.where(at // nvec == to // width, jnp.concatenate([charge] * (LANES // nvec), axis=0), 0.0)
             for charge in charged])
         whole = dot(exchange, above(*split_pair(blocks)), (1, 1))
-        for first_t in range(nb // 2, nb, group):
+        early = unfold(0, nv // 2)
+        for first_t in range(nb // 2, nb - nc, group):
             sums_t = [None] * group
             for l in range(levels):
                 for u in range(group):
@@ -381,9 +386,16 @@
                     sums_t[u] = term if l == 0 else sums_t[u] + term
             for u in range(group):
                 moved[first_t + u] = sums_t[u]
-        placed = jnp.concatenate(
-            [jnp.concatenate([moved[j * nc + c] for c in range(nc)], axis=0) for j in range(nv)], axis=1)
-        whole = whole + dot(select[:, 0:nv * LANES], above(*split_pair(placed)), (1, 1))
+        early = early + unfold(nv // 2, nv - 1)
+        for first_t in range(nb - nc, nb, group):
+            sums_t = [None] * group
+            for l in range(levels):
+                for u in range(group):
+                    term = pairs[first_t + u, l:l + 1, :] * proj[l]
+                    sums_t[u] = term if l == 0 else sums_t[u] + term
+            for u in range(group):
+                moved[first_t + u] = sums_t[u]
+        whole = whole + early + unfold(nv - 1, nv)
         whole = whole[:, 0:LANES] + whole[:, LANES:]
         out_send[...] = whole.reshape(count, 8, LANES)
         start_all(out_copy, leading)

time: 18.7 us -> 18.7 us (level)
  no operation moved by 1% of the time
where the time goes in v6:
time: 18.7 us; the launch traced here: 18.5 us
  Pallas kernels  17.8 us (95%)
  between operations  0.64 us (3%)
    pallas_call x1, Pallas kernels, fast_on_device(): pl.pallas_call(functools.partial(kernel, (rows, cols, nk, nv, nc, nvec, t...  17.2 us
    pallas_call x1, Pallas kernels, fast_on_device(): pl.pallas_call(finish, out_shape=(jax.ShapeDtypeStruct((nk, nb * nvec), F...  0.63 us

profile of v6, /device:TPU:0, one launch (start us, length us, event | category | flops | bytes accessed | tf_op | source)
XLA Modules:
  0.0 18.5 jit_solution(3416375975236458375)
XLA Ops:
  0.6 17.2 %shard_map.95 = (f32[2,512]{1,0:T(2,128)S(1)}, f32[32,32]{1,0:T(8,128)S(1)}) custom-call(bf16[2,16,1024]{2,1,0:T(8,128)(2,1)} %px_hbm.1, bf16[2,4,1024]{2,1,0:T(4,128)(2,1)} %cond_hbm.1, bf16[2,4,1024]{2,1,0:T(4,128)(2,1)} %val_hbm.1, f32[1,1024]{1,0:T(1,128)} %bitcast.1, f32[34,1024]{1,0:T(8,128)} %screening_hbm.1, bf16[2,512]{1,0:T(2,128)(2,1)} %vec_hbm.1, ...), custom_call_target="tpu_custom_call" | custom-call | tf_op jit(solution)/shard_map/pallas_call | solution.py:469
  17.8 0.6 %shard_map.96 = (f32[2,512]{1,0:T(2,128)}, f32[32,32]{1,0:T(8,128)}) custom-call(f32[2,512]{1,0:T(2,128)S(1)} %get-tuple-element.4.out_ref, f32[32,32]{1,0:T(8,128)S(1)} %get-tuple-element.5.alpha_ref), custom_call_target="tpu_custom_call" | custom-call | tf_op jit(solution)/shard_map/pallas_call | solution.py:506

commit v7 on v6

--- a/solution.py
+++ b/solution.py
@@ -348,7 +348,8 @@
         scaled = spectral * spectrum[:, None, :]
         sides = [
             split_pair(jnp.concatenate([side[l] for l in range(levels)], axis=1)) for side in (spectral, scaled)]
-        gram = wide_dot(*sides, (1, 1))
+        stacked = dot(above(*sides[0]), sides[1][0], (1, 1))
+        gram = stacked[0:nvec] + stacked[nvec:] + dot(sides[0][0], sides[1][1], (1, 1))
 
         landed(px_slots.at[0:count - 1], arrivals.at[1])
         taken_px = px_slots[...].astype(F32)

time: 18.7 us -> 18.7 us (level)
  no operation moved by 1% of the time
where the time goes in v7:
time: 18.7 us; the launch traced here: 18.5 us
  Pallas kernels  17.8 us (95%)
  between operations  0.64 us (3%)
    pallas_call x1, Pallas kernels, fast_on_device(): pl.pallas_call(functools.partial(kernel, (rows, cols, nk, nv, nc, nvec, t...  17.2 us
    pallas_call x1, Pallas kernels, fast_on_device(): pl.pallas_call(finish, out_shape=(jax.ShapeDtypeStruct((nk, nb * nvec), F...  0.63 us

profile of v7, /device:TPU:0, one launch (start us, length us, event | category | flops | bytes accessed | tf_op | source)
XLA Modules:
  0.0 18.5 jit_solution(1223088722900014990)
XLA Ops:
  0.6 17.2 %shard_map.95 = (f32[2,512]{1,0:T(2,128)S(1)}, f32[32,32]{1,0:T(8,128)S(1)}) custom-call(bf16[2,16,1024]{2,1,0:T(8,128)(2,1)} %px_hbm.1, bf16[2,4,1024]{2,1,0:T(4,128)(2,1)} %cond_hbm.1, bf16[2,4,1024]{2,1,0:T(4,128)(2,1)} %val_hbm.1, f32[1,1024]{1,0:T(1,128)} %bitcast.1, f32[34,1024]{1,0:T(8,128)} %screening_hbm.1, bf16[2,512]{1,0:T(2,128)(2,1)} %vec_hbm.1, ...), custom_call_target="tpu_custom_call" | custom-call | tf_op jit(solution)/shard_map/pallas_call | solution.py:470
  17.8 0.6 %shard_map.96 = (f32[2,512]{1,0:T(2,128)}, f32[32,32]{1,0:T(8,128)}) custom-call(f32[2,512]{1,0:T(2,128)S(1)} %get-tuple-element.4.out_ref, f32[32,32]{1,0:T(8,128)S(1)} %get-tuple-element.5.alpha_ref), custom_call_target="tpu_custom_call" | custom-call | tf_op jit(solution)/shard_map/pallas_call | solution.py:507

commit v8 on v7

--- a/solution.py
+++ b/solution.py
@@ -102,7 +102,7 @@
     host_rows = [low_row + lax.rem(near_row - low_row + step, high_row - low_row) for step in range(high_row - low_row)]
     left = lax.rem(col, 2)
     host_cols = [cols - 1 - col, lax.rem(col + 2, cols), col + 1 - 2 * left, col]
-    host_peers = [(pr, pc) for pc in host_cols for pr in host_rows[::-1]]
+    host_peers = [(pr, pc) for pc in [host_cols[0], host_cols[2], host_cols[1], host_cols[3]] for pr in [host_rows[2], host_rows[3], host_rows[1], host_rows[0]]]
 
     barrier = pltpu.get_barrier_semaphore()
     mine = pl.ds(pl.multiple_of(seat // 2 * LANES, LANES), LANES)

time: 18.7 us -> 18.6 us (level)
  no operation moved by 1% of the time
where the time goes in v8:
time: 18.6 us; the launch traced here: 18.4 us
  Pallas kernels  17.7 us (95%)
  between operations  0.64 us (3%)
    pallas_call x1, Pallas kernels, fast_on_device(): pl.pallas_call(functools.partial(kernel, (rows, cols, nk, nv, nc, nvec, t...  17.1 us
    pallas_call x1, Pallas kernels, fast_on_device(): pl.pallas_call(finish, out_shape=(jax.ShapeDtypeStruct((nk, nb * nvec), F...  0.63 us

profile of v8, /device:TPU:0, one launch (start us, length us, event | category | flops | bytes accessed | tf_op | source)
XLA Modules:
  0.0 18.4 jit_solution(10985863806842963962)
XLA Ops:
  0.6 17.1 %shard_map.95 = (f32[2,512]{1,0:T(2,128)S(1)}, f32[32,32]{1,0:T(8,128)S(1)}) custom-call(bf16[2,16,1024]{2,1,0:T(8,128)(2,1)} %px_hbm.1, bf16[2,4,1024]{2,1,0:T(4,128)(2,1)} %cond_hbm.1, bf16[2,4,1024]{2,1,0:T(4,128)(2,1)} %val_hbm.1, f32[1,1024]{1,0:T(1,128)} %bitcast.1, f32[34,1024]{1,0:T(8,128)} %screening_hbm.1, bf16[2,512]{1,0:T(2,128)(2,1)} %vec_hbm.1, ...), custom_call_target="tpu_custom_call" | custom-call | tf_op jit(solution)/shard_map/pallas_call | solution.py:470
  17.7 0.6 %shard_map.96 = (f32[2,512]{1,0:T(2,128)}, f32[32,32]{1,0:T(8,128)}) custom-call(f32[2,512]{1,0:T(2,128)S(1)} %get-tuple-element.4.out_ref, f32[32,32]{1,0:T(8,128)S(1)} %get-tuple-element.5.alpha_ref), custom_call_target="tpu_custom_call" | custom-call | tf_op jit(solution)/shard_map/pallas_call | solution.py:507
